TPU v7x, 256 devices: a whole 4x4x8 slice. The times are simulated.
256 devices in a mesh: sph: 256 (over x, y, z, core).
Axes of the slice: x: 4, y: 4, z: 8, core: 2. Of those that a mesh axis runs over, the one named last changes fastest.
Arguments:
- right_side: float32 [4096, 2, 336], P('sph'), may hold values from -8 to 8
- positions: float32 [3, 4096], P(None, 'sph'), may hold values from -0.1 to 15.1, as said below
- sphere_radii: float32 [4096], P('sph'), may hold values from 0.2 to 0.35
- azimuths: float32 [4096], P('sph'), may hold values from -3.1416 to 3.1416
- pair_flags: int32 [4096, 4096], P('sph'), may hold values from 0 to 2, as said below
- pair_counts: int32 [4096], P('sph'), may hold values from 1 to 4095, as said below
- tilt_matrix: float32 [336, 336], replicated, may hold values from -1 to 1
- axial_terms: float32 [8, 336, 336], replicated, may hold values from -1 to 1
Outputs:
- solution: float32 [4096, 2, 336], P('sph')
- residual: float32 [4096, 2, 336], P('sph')
- direction: float32 [4096, 2, 336], P('sph')
Inputs may be any that keep to these rules, and one draw needn't show every extreme that they name: pair_flags is symmetric and zero on the diagonal. pair_counts[i] is the number of j with pair_flags[i, j] != 0; one sphere is linked to every other. `positions`: any two sphere centres are at least 0.8 apart.
All inputs are finite; a program needn't handle non-finite values.
Results may differ from a plain program's by a relative error of at most 0.0003.
Values sent between devices are 32-bit elements; how exact they have to be, the bound alone decides.
A program may use at most 64 MiB of HBM per device.

v0:
```python
import jax
import jax.numpy as jnp
import numpy as np
from jax import lax
from jax.sharding import Mesh
from jax.sharding import PartitionSpec as P

DEG = 12
TERMS = 8
SPH = ("sph_0", "sph_1", "sph_2", "sph_3")


coupling = 0.25
wavenum = 2.5
phase_step = 0.9
dist_floor = 0.8


def joined_along(parts, dim):
    parts = jnp.moveaxis(parts, 0, dim)
    shape = parts.shape
    return parts.reshape(*shape[:dim], shape[dim] * shape[dim + 1], *shape[dim + 2 :])


def stacked_from(x, axes, turns):
    parts = x
    for k in turns:
        parts = lax.all_gather(parts, axes[k])
    done = turns[::-1]
    back = [done.index(k) for k in range(len(axes))]
    parts = parts.transpose(*back, *range(len(axes), parts.ndim))
    return parts.reshape(-1, *x.shape)


def gather_axes(x, axes, turns, dim):
    return joined_along(stacked_from(x, axes, turns), dim)


def from_partner(value, axis, apart):
    mask = 2**apart
    pairs = [(source, source ^ mask) for source in range(lax.axis_size(axis))]
    return lax.ppermute(value, axis, pairs)


def by_axis(x, axes):
    for axis in axes:
        x = lax.psum(x, axis)
    return x


def orders_table():
    return np.concatenate([np.arange(-degree, degree + 1) for degree in range(1, DEG + 1)]).astype(
        np.float32
    )


def rotate_z(vector, azimuth, handed):
    half_len = vector.shape[-1] // 2
    phases = azimuth[:, None] * jnp.asarray(orders_table())[None, :]
    cosine = jnp.cos(phases)[:, None, :]
    sine_part = handed * jnp.sin(phases)[:, None, :]
    real_part = vector[..., :half_len]
    imag_part = vector[..., half_len:]
    return jnp.concatenate(
        [cosine * real_part - sine_part * imag_part, sine_part * real_part + cosine * imag_part],
        axis=-1,
    )


def pair_weights(flag_block, geo_rows, geo_cols):
    delta_x = geo_rows[0][:, None] - geo_cols[0][None, :]
    delta_y = geo_rows[1][:, None] - geo_cols[1][None, :]
    delta_z = geo_rows[2][:, None] - geo_cols[2][None, :]
    distance = jnp.sqrt(delta_x * delta_x + delta_y * delta_y + delta_z * delta_z)
    size_ratio = (geo_rows[3][:, None] + geo_cols[3][None, :]) / jnp.maximum(distance, dist_floor)
    linked = (flag_block != 0).astype(distance.dtype)
    nearby = (flag_block == 1).astype(distance.dtype)
    ratio_power = jnp.ones_like(distance)
    weights = []
    for term_index in range(TERMS):
        selector = linked if term_index == 0 else nearby
        weights.append(
            coupling
            * ratio_power
            * jnp.cos(wavenum * distance + phase_step * term_index)
            * selector
        )
        ratio_power = ratio_power * size_ratio
    return jnp.stack(weights)


def to_frame(vector, azimuths, tilt_matrix):
    return jnp.einsum(
        "spk,kl->spl", rotate_z(vector, azimuths, 1.0), tilt_matrix, precision=lax.Precision.HIGHEST
    )


def from_frame(coupled, azimuths, tilt_matrix, pair_counts):
    unturned = jnp.einsum("spl,kl->spk", coupled, tilt_matrix, precision=lax.Precision.HIGHEST)
    inverse_root = 1.0 / jnp.sqrt(1.0 + pair_counts.astype(jnp.float32))
    return rotate_z(unturned * inverse_root[:, None, None], azimuths, -1.0)


def inner(left, right):
    return jnp.sum(left * right)


def pick_half(array, which, axis_index):
    return lax.dynamic_index_in_dim(array, which, axis_index, keepdims=False)


def on_device(
    right_side, positions, sphere_radii, azimuths, pair_flags, pair_counts, tilt_matrix, axial_terms
):
    sph_dev = right_side.shape[0]
    geometry = jnp.concatenate([positions, sphere_radii[None, :]], axis=0)
    geo_all = gather_axes(geometry, SPH, (0, 1, 2, 3), 1)
    lanes = lax.axis_size(SPH)
    level_bits = lanes.bit_length() - 1
    groups = lanes // 16
    group_width = 16 * sph_dev
    my_index = lax.axis_index(SPH)
    lane_q = my_index % 16
    lane_g = my_index // 16
    stripe_flags = pair_flags.reshape(sph_dev, groups, group_width)
    for level in range(4, level_bits):
        own_bit = my_index >> level & 1
        current = stripe_flags.shape[1]
        split_flags = stripe_flags.reshape(stripe_flags.shape[0], current // 2, 2, group_width)
        kept_flags = pick_half(split_flags, own_bit, 2)
        sent_flags = pick_half(split_flags, 1 - own_bit, 2)
        got_flags = from_partner(sent_flags, SPH, level)
        stripe_flags = jnp.where(
            own_bit == 0,
            jnp.concatenate([kept_flags, got_flags], 0),
            jnp.concatenate([got_flags, kept_flags], 0),
        )
    stripe_flags = stripe_flags.reshape(-1, group_width)
    geo_sources = pick_half(geo_all.reshape(4, groups, 16, sph_dev), lane_q, 2).reshape(
        4, groups * sph_dev
    )
    geo_targets = lax.dynamic_slice_in_dim(geo_all, lane_g * group_width, group_width, 1)
    grid_weights = pair_weights(stripe_flags.T, geo_targets, geo_sources)

    def apply_op(vector):
        framed = to_frame(vector, azimuths, tilt_matrix)
        stripe = framed.reshape(sph_dev, -1)
        for level in range(4, level_bits):
            own_bit = my_index >> level & 1
            got_rows = from_partner(stripe, SPH, level)
            stripe = jnp.where(
                own_bit == 0,
                jnp.concatenate([stripe, got_rows], 0),
                jnp.concatenate([got_rows, stripe], 0),
            )
        gathered = jnp.einsum("mtj,jk->mtk", grid_weights, stripe, precision=lax.Precision.HIGHEST)
        gathered = gathered.reshape(TERMS, group_width, 2, -1)
        partial_field = jnp.einsum(
            "mtpk,mkl->tpl", gathered, axial_terms, precision=lax.Precision.HIGHEST
        )
        partial_field = partial_field.reshape(16, sph_dev, 2, -1)
        for level in (3, 2, 1, 0):
            own_bit = my_index >> level & 1
            split_field = partial_field.reshape(2, partial_field.shape[0] // 2, sph_dev, 2, -1)
            kept_field = pick_half(split_field, own_bit, 0)
            sent_field = pick_half(split_field, 1 - own_bit, 0)
            partial_field = kept_field + from_partner(sent_field, SPH, level)
        coupled = partial_field
        coupled = coupled.reshape(vector.shape)
        return vector - from_frame(coupled, azimuths, tilt_matrix, pair_counts)

    image_p = apply_op(right_side)
    rho_start, along_v = (
        by_axis(inner(right_side, right_side), SPH),
        by_axis(inner(right_side, image_p), SPH),
    )
    step_alpha = rho_start / along_v
    half_step = right_side - step_alpha * image_p
    half_image = apply_op(half_step)
    t_dot_s, t_dot_t, shadow_s, shadow_t = (
        by_axis(inner(half_image, half_step), SPH),
        by_axis(inner(half_image, half_image), SPH),
        by_axis(inner(right_side, half_step), SPH),
        by_axis(inner(right_side, half_image), SPH),
    )
    step_omega = t_dot_s / t_dot_t
    rho_next = shadow_s - step_omega * shadow_t
    solution = step_alpha * right_side + step_omega * half_step
    residual = half_step - step_omega * half_image
    step_beta = rho_next / rho_start * (step_alpha / step_omega)
    direction = residual + step_beta * (right_side - step_omega * image_p)
    return (solution, residual, direction)


def solution(mesh):
    split = Mesh(mesh.devices.reshape(4, 4, 8, 2), ("sph_0", "sph_1", "sph_2", "sph_3"))
    placed = (P(SPH, None, None), P(None, SPH), P(SPH), P(SPH), P(SPH, None), P(SPH), P(), P())
    return jax.shard_map(
        on_device,
        mesh=split,
        in_specs=placed,
        out_specs=(P(SPH, None, None), P(SPH, None, None), P(SPH, None, None)),
        check_vma=False,
    )
```

profile of v0, /device:TPU:1, one launch (start us, length us, event | category | flops | bytes accessed | tf_op | source)
XLA Modules:
  0.0 343.6 jit_solution(2390027228763923636)
XLA Ops:
  0.7 1.2 reshape_reshape.8
  2.2 2.2 collective-permute-start
  7.0 3.6 %collective-permute-start.1 = (s32[32,4,256]{2,0,1:T(8,128)S(1)}, s32[32,4,256]{2,0,1:T(8,128)S(1)}, u32[]{:S(2)}, u32[]{:S(2)}) collective-permute-start(s32[32,4,256]{2,0,1:T(8,128)S(1)} %get-tuple-element.61), channel_id=1, source_target_pairs={{0,32},{1,33},{2,34},{3,35},{4,36},{5,37},{6,38},{7,39},{8,40},{9,... | collective-permute-start | bytes 393224 | tf_op jit(solution)/shard_map/ppermute | solution.py:42
  10.6 8.5 %all-gather.4 = f32[4,4,16]{2,1,0:T(4,128)S(1)} all-gather(f32[1,4,16]{2,1,0:T(4,128)S(1)} %maximum_bitcast_fusion), channel_id=2, replica_groups=mesh['sph_0'=4,'sph_1'=4,'sph_2'=8,'sph_3'=2] {'sph_0'}, dimensions={0}, use_global_device_ids=true | all-gather | bytes 1280 | tf_op jit(solution)/shard_map/all_gather | solution.py:28
  19.1 9.0 %all-gather.1 = f32[16,4,16]{2,1,0:T(4,128)S(1)} all-gather(f32[4,4,16]{2,1,0:T(4,128)S(1)} %all-gather.4), channel_id=3, replica_groups=mesh['sph_0'=4,'sph_1'=4,'sph_2'=8,'sph_3'=2] {'sph_1'}, dimensions={0}, use_global_device_ids=true | all-gather | bytes 5120 | tf_op jit(solution)/shard_map/all_gather | solution.py:28
  28.1 22.0 %all-gather.2 = f32[32,4,4,16]{3,2,1,0:T(4,128)S(1)} all-gather(f32[4,4,4,16]{3,2,1,0:T(4,128)S(1)} %bitcast.171), channel_id=4, replica_groups=mesh['sph_0'=4,'sph_1'=4,'sph_2'=8,'sph_3'=2] {'sph_2'}, dimensions={0}, use_global_device_ids=true | all-gather | bytes 36864 | tf_op jit(solution)/shard_map/all_gather | solution.py:28
  50.3 1.3 collective-permute-start.5
  51.7 1.6 collective-permute-start.2
  53.3 15.5 %all-gather.3 = f32[16,4,4,4,16]{4,1,0,3,2:T(4,128)S(1)} all-gather(f32[8,4,4,4,16]{4,1,0,3,2:T(4,128)S(1)} %bitcast.158), channel_id=5, replica_groups=mesh['sph_0'=4,'sph_1'=4,'sph_2'=8,'sph_3'=2] {'sph_3'}, dimensions={0}, use_global_device_ids=true | all-gather | bytes 98304 | tf_op jit(solution)/shard_map/all_gather | solution.py:28
  70.5 1.9 collective-permute-start.3
  72.9 2.5 collective-permute-done.6
  75.4 2.0 collective-permute-start.7
  79.5 1.5 bitcast_dynamic-update-slice_fusion
  81.0 1.4 fusion.72
  82.4 1.4 fusion.68
  83.9 1.5 fusion.64
  85.4 1.5 fusion.60
  86.8 1.5 fusion.51
  88.3 1.5 fusion.56
  89.8 6.8 %fusion.17 = f32[8,256,672]{1,2,0:T(8,128)} fusion(f32[8,256,256]{2,1,0:T(8,128)S(1)} %fusion.56, f32[128,672]{1,0:T(8,128)S(1)} %collective-permute-done.7, f32[128,672]{1,0:T(8,128)S(1)} %maximum_select_fusion.2, pred[]{:T(512)S(6)} %eq.31), kind=kOutput, calls=%fused_computation.12 | convolution fusion | flops 4228374528 | bytes 8290305 | tf_op jit(solution)/shard_map/mtj,jk->mtk/dot_general | solution.py:156
  96.6 6.6 %copy.136 = f32[8,256,2,336]{3,0,2,1:T(8,128)} copy(f32[8,256,2,336]{1,3,2,0:T(8,128)} %bitcast.148) | data formatting | bytes 11010048 | tf_op jit(solution)/shard_map/reshape | solution.py:157
  103.1 15.6 %fusion.6 = f32[2,8,16,2,336]{4,2,3,1,0:T(8,128)S(1)} fusion(f32[8,336,336]{2,1,0:T(8,128)} %param.19, f32[2,8,16,2,336,8]{4,5,3,2,1,0:T(8,128)} %bitcast.149), kind=kOutput, calls=%fused_computation.6 | convolution fusion | flops 5549064192 | bytes 9805824 | tf_op jit(solution)/shard_map/mtpk,mkl->tpl/dot_general | solution.py:158
  119.6 3.4 collective-permute-start.8
  123.0 19.3 %collective-permute-done.8 = f32[8,16,2,336]{3,1,2,0:T(8,128)} collective-permute-done((f32[8,16,2,336]{3,1,2,0:T(8,128)S(1)}, f32[8,16,2,336]{3,1,2,0:T(8,128)}, u32[]{:S(2)}, u32[]{:S(2)}) %collective-permute-start.8) | collective-permute-done | bytes 344096 | tf_op jit(solution)/shard_map/ppermute | solution.py:42
  142.3 1.2 bitcast_add_fusion.1
  143.6 11.2 %collective-permute-done.9 = f32[4,16,2,336]{3,1,2,0:T(8,128)S(1)} collective-permute-done((f32[4,16,2,336]{3,1,2,0:T(8,128)S(1)}, f32[4,16,2,336]{3,1,2,0:T(8,128)S(1)}, u32[]{:S(2)}, u32[]{:S(2)}) %collective-permute-start.9) | collective-permute-done | bytes 172064 | tf_op jit(solution)/shard_map/ppermute | solution.py:42
  155.0 3.8 %collective-permute-done.10 = f32[2,16,2,336]{3,1,2,0:T(8,128)S(1)} collective-permute-done((f32[2,16,2,336]{3,1,2,0:T(8,128)S(1)}, f32[2,16,2,336]{3,1,2,0:T(8,128)S(1)}, u32[]{:S(2)}, u32[]{:S(2)}) %collective-permute-start.10) | collective-permute-done | bytes 86048 | tf_op jit(solution)/shard_map/ppermute | solution.py:42
  158.9 1.4 collective-permute-start.11
  162.6 8.8 %all-reduce.5 = (f32[]{:T(128)}, f32[]{:T(128)}) all-reduce(f32[]{:T(128)} %multiply_reduce_fusion.5, f32[]{:T(128)} %multiply_reduce_fusion.4), channel_id=1, replica_groups=mesh['sph_0'=4,'sph_1'=4,'sph_2'=8,'sph_3'=2] {'sph_0'}, use_global_device_ids=true, to_apply=%region_1.2 | all-reduce | flops 2 | bytes 16 | tf_op jit(solution)/shard_map/psum | solution.py:47
  171.4 7.6 %all-reduce.3 = (f32[]{:T(128)}, f32[]{:T(128)}) all-reduce(f32[]{:T(128)} %get-tuple-element.45, f32[]{:T(128)} %get-tuple-element.46), channel_id=1, replica_groups=mesh['sph_0'=4,'sph_1'=4,'sph_2'=8,'sph_3'=2] {'sph_1'}, use_global_device_ids=true, to_apply=%region_2.3 | all-reduce | flops 2 | bytes 16 | tf_op jit(solution)/shard_map/psum | solution.py:47
  179.0 12.8 %all-reduce.1 = (f32[]{:T(128)}, f32[]{:T(128)}) all-reduce(f32[]{:T(128)} %get-tuple-element.39, f32[]{:T(128)} %get-tuple-element.40), channel_id=1, replica_groups=mesh['sph_0'=4,'sph_1'=4,'sph_2'=8,'sph_3'=2] {'sph_2'}, use_global_device_ids=true, to_apply=%region_3.4 | all-reduce | flops 2 | bytes 16 | tf_op jit(solution)/shard_map/psum | solution.py:47
  191.8 10.9 %all-reduce.7 = (f32[]{:T(128)}, f32[]{:T(128)}) all-reduce(f32[]{:T(128)} %get-tuple-element.33, f32[]{:T(128)} %get-tuple-element.34), channel_id=1, replica_groups=mesh['sph_0'=4,'sph_1'=4,'sph_2'=8,'sph_3'=2] {'sph_3'}, use_global_device_ids=true, to_apply=%region_4.5 | all-reduce | flops 2 | bytes 16 | tf_op jit(solution)/shard_map/psum | solution.py:47
  205.2 2.6 collective-permute-done.12
  208.5 4.4 %collective-permute-done.13 = f32[32,672]{1,0:T(8,128)S(1)} collective-permute-done((f32[32,672]{1,0:T(8,128)S(1)}, f32[32,672]{1,0:T(8,128)S(1)}, u32[]{:S(2)}, u32[]{:S(2)}) %collective-permute-start.13) | collective-permute-done | bytes 86048 | tf_op jit(solution)/shard_map/ppermute | solution.py:42
  213.0 4.5 %collective-permute-done.14 = f32[64,672]{1,0:T(8,128)S(1)} collective-permute-done((f32[64,672]{1,0:T(8,128)S(1)}, f32[64,672]{1,0:T(8,128)S(1)}, u32[]{:S(2)}, u32[]{:S(2)}) %collective-permute-start.14) | collective-permute-done | bytes 172064 | tf_op jit(solution)/shard_map/ppermute | solution.py:42
  218.4 7.6 %collective-permute-done.15 = f32[128,672]{1,0:T(8,128)S(1)} collective-permute-done((f32[128,672]{1,0:T(8,128)S(1)}, f32[128,672]{1,0:T(8,128)S(1)}, u32[]{:S(2)}, u32[]{:S(2)}) %collective-permute-start.15) | collective-permute-done | bytes 344096 | tf_op jit(solution)/shard_map/ppermute | solution.py:42
  225.9 6.4 %fusion.25 = f32[8,256,672]{1,2,0:T(8,128)} fusion(f32[8,256,256]{2,1,0:T(8,128)S(1)} %fusion.56, f32[128,672]{1,0:T(8,128)S(1)} %collective-permute-done.15, f32[128,672]{1,0:T(8,128)S(1)} %maximum_select_fusion.3, pred[]{:T(512)S(6)} %eq.31), kind=kOutput, calls=%fused_computation.20 | convolution fusion | flops 4228374528 | bytes 8290305 | tf_op jit(solution)/shard_map/mtj,jk->mtk/dot_general | solution.py:156
  232.3 6.6 %copy.144 = f32[8,256,2,336]{3,0,2,1:T(8,128)} copy(f32[8,256,2,336]{1,3,2,0:T(8,128)} %bitcast.147) | data formatting | bytes 11010048 | tf_op jit(solution)/shard_map/reshape | solution.py:157
  238.9 15.6 %fusion.11 = f32[2,8,16,2,336]{4,2,3,1,0:T(8,128)S(1)} fusion(f32[8,336,336]{2,1,0:T(8,128)} %param.19, f32[2,8,16,2,336,8]{4,5,3,2,1,0:T(8,128)} %bitcast.150), kind=kOutput, calls=%fused_computation.7 | convolution fusion | flops 5549064192 | bytes 9805824 | tf_op jit(solution)/shard_map/mtpk,mkl->tpl/dot_general | solution.py:158
  254.5 2.5 collective-permute-start.16
  257.1 15.0 %collective-permute-done.16 = f32[8,16,2,336]{3,1,2,0:T(8,128)S(1)} collective-permute-done((f32[8,16,2,336]{3,1,2,0:T(8,128)S(1)}, f32[8,16,2,336]{3,1,2,0:T(8,128)S(1)}, u32[]{:S(2)}, u32[]{:S(2)}) %collective-permute-start.16) | collective-permute-done | bytes 344096 | tf_op jit(solution)/shard_map/ppermute | solution.py:42
  272.2 9.4 %collective-permute-done.17 = f32[4,16,2,336]{3,1,2,0:T(8,128)S(1)} collective-permute-done((f32[4,16,2,336]{3,1,2,0:T(8,128)S(1)}, f32[4,16,2,336]{3,1,2,0:T(8,128)S(1)}, u32[]{:S(2)}, u32[]{:S(2)}) %collective-permute-start.17) | collective-permute-done | bytes 172064 | tf_op jit(solution)/shard_map/ppermute | solution.py:42
  281.8 3.6 %collective-permute-done.18 = f32[2,16,2,336]{3,1,2,0:T(8,128)S(1)} collective-permute-done((f32[2,16,2,336]{3,1,2,0:T(8,128)S(1)}, f32[2,16,2,336]{3,1,2,0:T(8,128)S(1)}, u32[]{:S(2)}, u32[]{:S(2)}) %collective-permute-start.18) | collective-permute-done | bytes 86048 | tf_op jit(solution)/shard_map/ppermute | solution.py:42
  285.4 5.4 %collective-permute-start.19 = (f32[1,16,2,336]{3,1,2,0:T(8,128)S(1)}, f32[1,16,2,336]{3,1,2,0:T(8,128)S(1)}, u32[]{:S(2)}, u32[]{:S(2)}) collective-permute-start(f32[1,16,2,336]{3,1,2,0:T(8,128)S(1)} %constant_dynamic-slice_fusion.1), channel_id=1, source_target_pairs={{0,1},{1,0},{2,3},{3,2},{4,5},{5,4},{6,7},{7,6},{8,9},{9,8},{10,11... | collective-permute-start | bytes 129032 | tf_op jit(solution)/shard_map/ppermute | solution.py:42
  293.1 13.1 %all-reduce.4 = (f32[]{:T(128)}, f32[]{:T(128)}, f32[]{:T(128)}, f32[]{:T(128)}) all-reduce(f32[]{:T(128)} %get-tuple-element.27, f32[]{:T(128)} %get-tuple-element.28, f32[]{:T(128)} %get-tuple-element.26, f32[]{:T(128)} %get-tuple-element.25), channel_id=1, replica_groups=mesh['sph_0'=4,'sph_1'=4,'sph_2'=8,'sph_3'=2] {'sph_0'}, use_global_device_ids=true, to_apply=%region_11.12 | all-reduce | flops 4 | bytes 32 | tf_op jit(solution)/shard_map/psum | solution.py:47
  306.2 7.1 %all-reduce.2 = (f32[]{:T(128)}, f32[]{:T(128)}, f32[]{:T(128)}, f32[]{:T(128)}) all-reduce(f32[]{:T(128)} %get-tuple-element.41, f32[]{:T(128)} %get-tuple-element.42, f32[]{:T(128)} %get-tuple-element.43, f32[]{:T(128)} %get-tuple-element.44), channel_id=1, replica_groups=mesh['sph_0'=4,'sph_1'=4,'sph_2'=8,'sph_3'=2] {'sph_1'}, use_global_device_ids=true, to_apply=%region_12.13 | all-reduce | flops 4 | bytes 32 | tf_op jit(solution)/shard_map/psum | solution.py:47
  313.3 11.4 %all-reduce = (f32[]{:T(128)}, f32[]{:T(128)}, f32[]{:T(128)}, f32[]{:T(128)}) all-reduce(f32[]{:T(128)} %get-tuple-element.35, f32[]{:T(128)} %get-tuple-element.36, f32[]{:T(128)} %get-tuple-element.37, f32[]{:T(128)} %get-tuple-element.38), channel_id=1, replica_groups=mesh['sph_0'=4,'sph_1'=4,'sph_2'=8,'sph_3'=2] {'sph_2'}, use_global_device_ids=true, to_apply=%region_13.14 | all-reduce | flops 4 | bytes 32 | tf_op jit(solution)/shard_map/psum | solution.py:47
  324.7 10.9 %all-reduce.6 = (f32[]{:T(128)}, f32[]{:T(128)}, f32[]{:T(128)}, f32[]{:T(128)}) all-reduce(f32[]{:T(128)} %get-tuple-element.29, f32[]{:T(128)} %get-tuple-element.30, f32[]{:T(128)} %get-tuple-element.31, f32[]{:T(128)} %get-tuple-element.32), channel_id=1, replica_groups=mesh['sph_0'=4,'sph_1'=4,'sph_2'=8,'sph_3'=2] {'sph_3'}, use_global_device_ids=true, to_apply=%region_14.15 | all-reduce | flops 4 | bytes 32 | tf_op jit(solution)/shard_map/psum | solution.py:47
  (97 shorter events, 18.1 us)
Async XLA Ops:
  0.6 5.5 %copy-start = (f32[336,336]{1,0:T(8,128)S(1)}, f32[336,336]{1,0:T(8,128)}, u32[]{:S(2)}) copy-start(f32[336,336]{1,0:T(8,128)} %param.18) | copy-start | bytes 1354756
  0.6 6.2 %copy-start.4 = (f32[16]{0:T(128)S(1)}, f32[16]{0:T(128)}, u32[]{:S(2)}) copy-start(f32[16]{0:T(128)} %param.14) | copy-start | bytes 196
  0.7 6.2 %copy-start.3 = (f32[3,16]{1,0:T(4,128)S(1)}, f32[3,16]{1,0:T(4,128)}, u32[]{:S(2)}) copy-start(f32[3,16]{1,0:T(4,128)} %param.13) | copy-start | bytes 580
  2.2 4.7 %collective-permute-start = (s32[16,8,256]{2,1,0:T(8,128)S(1)}, s32[16,8,256]{2,1,0:T(8,128)S(1)}, u32[]{:S(2)}, u32[]{:S(2)}) collective-permute-start(s32[16,8,256]{2,1,0:T(8,128)S(1)} %bitcast.172), channel_id=1, source_target_pairs={{0,16},{1,17},{2,18},{3,19},{4,20},{5,21},{6,22},{7,23},{8,24},{9,... | collective-permute-start | bytes 393224 | tf_op jit(solution)/shard_map/ppermute | solution.py:42
  6.7 43.6 %collective-permute-start.4 = (f32[16,672]{1,0:T(8,128)S(1)}, f32[16,672]{1,0:T(8,128)S(1)}, u32[]{:S(2)}, u32[]{:S(2)}) collective-permute-start(f32[16,672]{1,0:T(8,128)S(1)} %reshape.282), channel_id=1, source_target_pairs={{0,16},{1,17},{2,18},{3,19},{4,20},{5,21},{6,22},{7,23},{8,24},{9,... | collective-permute-start | bytes 129032 | tf_op jit(solution)/shard_map/ppermute | solution.py:42
  7.0 44.5 %collective-permute-start.1 = (s32[32,4,256]{2,0,1:T(8,128)S(1)}, s32[32,4,256]{2,0,1:T(8,128)S(1)}, u32[]{:S(2)}, u32[]{:S(2)}) collective-permute-start(s32[32,4,256]{2,0,1:T(8,128)S(1)} %get-tuple-element.61), channel_id=1, source_target_pairs={{0,32},{1,33},{2,34},{3,35},{4,36},{5,37},{6,38},{7,39},{8,40},{9,... | collective-permute-start | bytes 393224 | tf_op jit(solution)/shard_map/ppermute | solution.py:42
  50.3 19.2 %collective-permute-start.5 = (f32[32,672]{1,0:T(8,128)S(1)}, f32[32,672]{1,0:T(8,128)S(1)}, u32[]{:S(2)}, u32[]{:S(2)}) collective-permute-start(f32[32,672]{1,0:T(8,128)S(1)} %maximum_select_fusion.6), channel_id=1, source_target_pairs={{0,32},{1,33},{2,34},{3,35},{4,36},{5,37},{6,38},{7,39},{8,40},{9,... | collective-permute-start | bytes 258056 | tf_op jit(solution)/shard_map/ppermute | solution.py:42
  51.7 18.5 %collective-permute-start.2 = (s32[64,2,256]{0,2,1:T(8,128)S(1)}, s32[64,2,256]{0,2,1:T(8,128)S(1)}, u32[]{:S(2)}, u32[]{:S(2)}) collective-permute-start(s32[64,2,256]{0,2,1:T(8,128)S(1)} %bitcast.169), channel_id=1, source_target_pairs={{0,64},{1,65},{2,66},{3,67},{4,68},{5,69},{6,70},{7,71},{8,72},{9,... | collective-permute-start | bytes 393224 | tf_op jit(solution)/shard_map/ppermute | solution.py:42
  69.5 5.8 %collective-permute-start.6 = (f32[64,672]{1,0:T(8,128)S(1)}, f32[64,672]{1,0:T(8,128)S(1)}, u32[]{:S(2)}, u32[]{:S(2)}) collective-permute-start(f32[64,672]{1,0:T(8,128)S(1)} %maximum_select_fusion.4), channel_id=1, source_target_pairs={{0,64},{1,65},{2,66},{3,67},{4,68},{5,69},{6,70},{7,71},{8,72},{9,... | collective-permute-start | bytes 516104 | tf_op jit(solution)/shard_map/ppermute | solution.py:42
  70.5 7.8 %collective-permute-start.3 = (s32[128,1,256]{0,2,1:T(8,128)S(1)}, s32[128,1,256]{0,2,1:T(8,128)S(1)}, u32[]{:S(2)}, u32[]{:S(2)}) collective-permute-start(s32[128,1,256]{0,2,1:T(8,128)S(1)} %get-tuple-element.56), channel_id=1, source_target_pairs={{0,128},{1,129},{2,130},{3,131},{4,132},{5,133},{6,134},{7,135},{8... | collective-permute-start | bytes 393224 | tf_op jit(solution)/shard_map/ppermute | solution.py:42
  75.4 14.4 %collective-permute-start.7 = (f32[128,672]{1,0:T(8,128)S(1)}, f32[128,672]{1,0:T(8,128)S(1)}, u32[]{:S(2)}, u32[]{:S(2)}) collective-permute-start(f32[128,672]{1,0:T(8,128)S(1)} %maximum_select_fusion.2), channel_id=1, source_target_pairs={{0,128},{1,129},{2,130},{3,131},{4,132},{5,133},{6,134},{7,135},{8... | collective-permute-start | bytes 1032200 | tf_op jit(solution)/shard_map/ppermute | solution.py:42
  118.7 0.9 copy-start.2
  119.6 35.4 %copy-start.5 = (s32[16]{0:T(128)S(1)}, s32[16]{0:T(128)}, u32[]{:S(2)}) copy-start(s32[16]{0:T(128)} %param.17) | copy-start | bytes 196
  119.6 40.7 %copy-start.1 = (f32[16,2,336]{2,1,0:T(2,128)S(1)}, f32[16,2,336]{2,1,0:T(2,128)}, u32[]{:S(2)}) copy-start(f32[16,2,336]{2,1,0:T(2,128)} %param.12) | copy-start | bytes 129028
  119.6 22.7 %collective-permute-start.8 = (f32[8,16,2,336]{3,1,2,0:T(8,128)S(1)}, f32[8,16,2,336]{3,1,2,0:T(8,128)}, u32[]{:S(2)}, u32[]{:S(2)}) collective-permute-start(f32[8,16,2,336]{3,1,2,0:T(8,128)S(1)} %dynamic-slice_bitcast_fusion.1), channel_id=1, source_target_pairs={{0,8},{1,9},{2,10},{3,11},{4,12},{5,13},{6,14},{7,15},{8,0},{9,1},... | collective-permute-start | bytes 1032200 | tf_op jit(solution)/shard_map/ppermute | solution.py:42
  143.5 11.3 %collective-permute-start.9 = (f32[4,16,2,336]{3,1,2,0:T(8,128)S(1)}, f32[4,16,2,336]{3,1,2,0:T(8,128)S(1)}, u32[]{:S(2)}, u32[]{:S(2)}) collective-permute-start(f32[4,16,2,336]{3,1,2,0:T(8,128)S(1)} %dynamic-slice_bitcast_fusion.3), channel_id=1, source_target_pairs={{0,4},{1,5},{2,6},{3,7},{4,0},{5,1},{6,2},{7,3},{8,12},{9,13},{10,... | collective-permute-start | bytes 516104 | tf_op jit(solution)/shard_map/ppermute | solution.py:42
  154.9 3.9 %collective-permute-start.10 = (f32[2,16,2,336]{3,1,2,0:T(8,128)S(1)}, f32[2,16,2,336]{3,1,2,0:T(8,128)S(1)}, u32[]{:S(2)}, u32[]{:S(2)}) collective-permute-start(f32[2,16,2,336]{3,1,2,0:T(8,128)S(1)} %dynamic-slice_bitcast_fusion.7), channel_id=1, source_target_pairs={{0,2},{1,3},{2,0},{3,1},{4,6},{5,7},{6,4},{7,5},{8,10},{9,11},{10,... | collective-permute-start | bytes 258056 | tf_op jit(solution)/shard_map/ppermute | solution.py:42
  158.9 2.3 collective-permute-start.11
  204.8 3.0 collective-permute-start.12
  207.8 5.1 %collective-permute-start.13 = (f32[32,672]{1,0:T(8,128)S(1)}, f32[32,672]{1,0:T(8,128)S(1)}, u32[]{:S(2)}, u32[]{:S(2)}) collective-permute-start(f32[32,672]{1,0:T(8,128)S(1)} %maximum_select_fusion.7), channel_id=1, source_target_pairs={{0,32},{1,33},{2,34},{3,35},{4,36},{5,37},{6,38},{7,39},{8,40},{9,... | collective-permute-start | bytes 258056 | tf_op jit(solution)/shard_map/ppermute | solution.py:42
  212.9 4.6 %collective-permute-start.14 = (f32[64,672]{1,0:T(8,128)S(1)}, f32[64,672]{1,0:T(8,128)S(1)}, u32[]{:S(2)}, u32[]{:S(2)}) collective-permute-start(f32[64,672]{1,0:T(8,128)S(1)} %maximum_select_fusion.5), channel_id=1, source_target_pairs={{0,64},{1,65},{2,66},{3,67},{4,68},{5,69},{6,70},{7,71},{8,72},{9,... | collective-permute-start | bytes 516104 | tf_op jit(solution)/shard_map/ppermute | solution.py:42
  217.5 8.4 %collective-permute-start.15 = (f32[128,672]{1,0:T(8,128)S(1)}, f32[128,672]{1,0:T(8,128)S(1)}, u32[]{:S(2)}, u32[]{:S(2)}) collective-permute-start(f32[128,672]{1,0:T(8,128)S(1)} %maximum_select_fusion.3), channel_id=1, source_target_pairs={{0,128},{1,129},{2,130},{3,131},{4,132},{5,133},{6,134},{7,135},{8... | collective-permute-start | bytes 1032200 | tf_op jit(solution)/shard_map/ppermute | solution.py:42
  254.5 17.5 %collective-permute-start.16 = (f32[8,16,2,336]{3,1,2,0:T(8,128)S(1)}, f32[8,16,2,336]{3,1,2,0:T(8,128)S(1)}, u32[]{:S(2)}, u32[]{:S(2)}) collective-permute-start(f32[8,16,2,336]{3,1,2,0:T(8,128)S(1)} %dynamic-slice_bitcast_fusion), channel_id=1, source_target_pairs={{0,8},{1,9},{2,10},{3,11},{4,12},{5,13},{6,14},{7,15},{8,0},{9,1},... | collective-permute-start | bytes 1032200 | tf_op jit(solution)/shard_map/ppermute | solution.py:42
  272.1 9.5 %collective-permute-start.17 = (f32[4,16,2,336]{3,1,2,0:T(8,128)S(1)}, f32[4,16,2,336]{3,1,2,0:T(8,128)S(1)}, u32[]{:S(2)}, u32[]{:S(2)}) collective-permute-start(f32[4,16,2,336]{3,1,2,0:T(8,128)S(1)} %dynamic-slice_bitcast_fusion.2), channel_id=1, source_target_pairs={{0,4},{1,5},{2,6},{3,7},{4,0},{5,1},{6,2},{7,3},{8,12},{9,13},{10,... | collective-permute-start | bytes 516104 | tf_op jit(solution)/shard_map/ppermute | solution.py:42
  281.7 3.7 %collective-permute-start.18 = (f32[2,16,2,336]{3,1,2,0:T(8,128)S(1)}, f32[2,16,2,336]{3,1,2,0:T(8,128)S(1)}, u32[]{:S(2)}, u32[]{:S(2)}) collective-permute-start(f32[2,16,2,336]{3,1,2,0:T(8,128)S(1)} %dynamic-slice_bitcast_fusion.6), channel_id=1, source_target_pairs={{0,2},{1,3},{2,0},{3,1},{4,6},{5,7},{6,4},{7,5},{8,10},{9,11},{10,... | collective-permute-start | bytes 258056 | tf_op jit(solution)/shard_map/ppermute | solution.py:42
  285.4 6.3 %collective-permute-start.19 = (f32[1,16,2,336]{3,1,2,0:T(8,128)S(1)}, f32[1,16,2,336]{3,1,2,0:T(8,128)S(1)}, u32[]{:S(2)}, u32[]{:S(2)}) collective-permute-start(f32[1,16,2,336]{3,1,2,0:T(8,128)S(1)} %constant_dynamic-slice_fusion.1), channel_id=1, source_target_pairs={{0,1},{1,0},{2,3},{3,2},{4,5},{5,4},{6,7},{7,6},{8,9},{9,8},{10,11... | collective-permute-start | bytes 129032 | tf_op jit(solution)/shard_map/ppermute | solution.py:42
where the time goes:
time: 350 us; the launch traced here: 344 us
  blocking collectives  138 us (39%)
  waiting for transfers between devices  85.9 us (25%)
  matrix products  46.4 us (13%)
  starting transfers between devices  28.4 us (8%)
  local copies, waits for them, and re-layouts  20.3 us (6%)
  other arithmetic  16.4 us (5%)
  between operations  8.58 us (2%)
    ppermute x20, waiting for transfers between devices, from_partner(): return lax.ppermute(value, axis, pairs)  85.9 us
    psum x8, blocking collectives, by_axis(): x = lax.psum(x, axis)  82.7 us
    all_gather x4, blocking collectives, stacked_from(): parts = lax.all_gather(parts, axes[k])  55.1 us
    dot_general x2, matrix products, apply_op(): jnp.einsum('mtpk,mkl->tpl', gathered, axial_terms, precision=lax.Precisio...  31.2 us
    ppermute x20, starting transfers between devices, from_partner(): return lax.ppermute(value, axis, pairs)  28.4 us
    reshape x2, local copies, waits for them, and re-layouts, apply_op(): gathered = gathered.reshape(TERMS, group_width, 2, -1)  13.1 us
    dot_general x2, matrix products, apply_op(): jnp.einsum('mtj,jk->mtk', grid_weights, stripe, precision=lax.Precision.H...  13.1 us
    unnamed x8, other arithmetic  9.88 us
  transfers between devices with their start and end apart: 20, of which 14 were waited for; matrix products, arithmetic and copies ran while one was open for 5% of the time, Pallas kernels for 0%

commit v1 on v0

v1 whole, which is shorter than its diff:
```python
import functools

import jax
import jax.numpy as jnp
import numpy as np
from jax import lax
from jax.experimental import pallas as pl
from jax.experimental.pallas import tpu as pltpu
from jax.sharding import Mesh
from jax.sharding import PartitionSpec as P

DEG = 12
TERMS = 8
SPH = ("sph_0", "sph_1", "sph_2", "sph_3")
NX, NY, NZ, NC = 4, 4, 8, 2
MESH = pl.DeviceIdType.MESH

coupling = 0.25
wavenum = 2.5
phase_step = 0.9
dist_floor = 0.8

SD = 16
HALF = 168
C = 336
CP = 384
LINE = NX * NY
SRC = LINE * NC * SD
TGT = NZ * SD
BF = jnp.bfloat16
F32 = jnp.float32


def orders_rows():
    orders = np.concatenate([np.arange(-degree, degree + 1) for degree in range(1, DEG + 1)])
    rows = np.zeros((8, CP), np.float32)
    rows[0, :HALF] = orders
    rows[0, HALF:C] = orders
    rows[1, :HALF] = 1.0
    rows[1, HALF:C] = -1.0
    return rows


def sincos(x):
    q = jnp.floor(x * (2.0 / np.pi) + 0.5)
    r = x - q * 1.5703125
    r = r - q * 4.83751296997070312e-4
    r = r - q * 7.54978995489188216e-8
    r2 = r * r
    s = r + r * r2 * (-1.6666654611e-1 + r2 * (8.3321608736e-3 + r2 * (-1.9515295891e-4)))
    c = 1.0 - 0.5 * r2 + r2 * r2 * (
        4.166664568298827e-2 + r2 * (-1.388731625493765e-3 + r2 * 2.443315711809948e-5)
    )
    quad = q - 4.0 * jnp.floor(q * 0.25)
    odd = (quad == 1.0) | (quad == 3.0)
    sin_sign = jnp.where(quad >= 2.0, -1.0, 1.0)
    cos_sign = jnp.where((quad == 1.0) | (quad == 2.0), -1.0, 1.0)
    return jnp.where(odd, c, s) * sin_sign, jnp.where(odd, s, c) * cos_sign


def split(x):
    high = x.astype(BF)
    return high, (x - high.astype(F32)).astype(BF)


def dot(a, b):
    return lax.dot_general(a, b, (((1,), (0,)), ((), ())), preferred_element_type=F32)


def dot_nt(a, b):
    return lax.dot_general(a, b, (((1,), (1,)), ((), ())), preferred_element_type=F32)


def lanes_of(x):
    total = jnp.sum(x, axis=0, keepdims=True)
    return total[:, 0:128] + total[:, 128:256] + total[:, 256:384]


def kernel(
    vec_ref, pos_ref, rad_ref, az_ref, flags_ref, counts_ref, tilt_ref, axial_hbm, rows_ref,
    sol_ref, res_ref, dir_ref,
    axial, ax_hi, ax_lo, tilt_hi, tilt_lo, flag_out, flag_in, mine, geo_src_out, geo_tgt_out,
    geo_src, geo_tgt, w_hi, w_lo, field, f_hi, f_lo, g_lhs, part, got, vec, img, img2,
    scal_out, scal_a, scal_mid, scal_b,
    ax_sem, geo_src_send, geo_src_recv, geo_tgt_send, geo_tgt_recv, flag_send, flag_recv,
    field_send, field_recv, pair_send, pair_recv, part_send, part_recv,
    sa_send, sa_recv, sb_send, sb_recv,
):
    mx, my, mz, mc = (lax.axis_index(name) for name in SPH)
    plane = mx * NY + my
    slot = plane * NC + mc

    def plane_peer(i):
        return (lax.rem(mx + i // NY, NX), lax.rem(my + lax.rem(i, NY), NY), mz, mc)

    def plane_source(i):
        return lax.rem(mx + NX - i // NY, NX) * NY + lax.rem(my + NY - lax.rem(i, NY), NY)

    def line_peer(j):
        return (mx, my, lax.rem(mz + j, NZ), mc)

    def pillar_peer(j):
        return (mx, my, lax.rem(mz + j // NC, NZ), lax.rem(mc + lax.rem(j, NC), NC))

    partner = (mx, my, mz, 1 - mc)

    def remote(src, dst, send, recv, peer):
        return pltpu.make_async_remote_copy(
            src_ref=src, dst_ref=dst, send_sem=send, recv_sem=recv, device_id=peer,
            device_id_type=MESH,
        )

    ax_copy = pltpu.make_async_copy(axial_hbm, axial, ax_sem)
    ax_copy.start()

    barrier = pltpu.get_barrier_semaphore()

    def greet_plane(i, carry):
        for core in range(NC):
            peer = plane_peer(i)
            pl.semaphore_signal(
                barrier, inc=1, device_id=(peer[0], peer[1], peer[2], core), device_id_type=MESH
            )
        return carry

    lax.fori_loop(1, LINE, greet_plane, 0)

    def greet_pillar(j, carry):
        pl.semaphore_signal(barrier, inc=1, device_id=pillar_peer(j), device_id_type=MESH)
        return carry

    lax.fori_loop(1, NZ * NC, greet_pillar, 0)

    mine[...] = jnp.zeros((8, 128), F32)
    mine[0:3, 0:SD] = pos_ref[...]
    mine[3:4, 0:SD] = rad_ref[...]
    mine[4:5, 0:SD] = az_ref[...]
    mine[5:6, 0:SD] = counts_ref[...].astype(F32)
    own = mine[...]
    lane = lax.broadcasted_iota(jnp.int32, (8, 128), 1)
    spread = own
    for shift in (16, 32, 64):
        spread = spread + pltpu.roll(spread, shift, 1)
    geo_src_out[...] = jnp.where(lane // SD == lax.rem(slot, 8), spread, 0.0)
    geo_tgt_out[...] = jnp.where(lane // SD == mz, spread, 0.0)
    geo_src[pl.ds(slot, 1)] = geo_src_out[...][None]
    geo_tgt[pl.ds(0, 1)] = geo_tgt_out[...][None]

    for z in range(NZ):
        r = z % 4
        for j in range(4):
            tile = None
            for i in range(4):
                at = ((4 * j + i) * 2 + z // 4) * 128
                piece = flags_ref[:, at : at + 128]
                if i != r:
                    piece = pltpu.roll(piece, (32 * (i - r)) % 128, 1)
                if tile is None:
                    tile = piece
                else:
                    where = lax.broadcasted_iota(jnp.int32, (SD, 128), 1) // 32 == i
                    tile = jnp.where(where, piece, tile)
            flag_out[z, :, 128 * j : 128 * (j + 1)] = tile

    cols = jnp.transpose(jnp.concatenate([own] * 16, axis=0))
    azimuth = cols[0:SD, 4:5]
    root = 1.0 / jnp.sqrt(1.0 + cols[0:SD, 5:6])
    sin_az, cos_az = sincos(azimuth * rows_ref[0:1, :])
    sin_az = sin_az * rows_ref[1:2, :]
    zeros_pad = jnp.zeros((CP - C, CP), BF)
    for half in range(2):
        for which, ref in enumerate((tilt_hi, tilt_lo)):
            ref[half * CP + C : half * CP + CP, :] = zeros_pad
    for half, (a, b) in enumerate(((0, HALF), (HALF, 0))):
        block = jnp.concatenate(
            [tilt_ref[a : a + HALF, :], tilt_ref[b : b + HALF, :]], axis=0
        )
        block = jnp.concatenate([block, jnp.zeros((C, CP - C), F32)], axis=1)
        high, low = split(block)
        tilt_hi[half * CP : half * CP + C, :] = high
        tilt_lo[half * CP : half * CP + C, :] = low

    def to_frame(x):
        high, low = split(jnp.concatenate([x * cos_az, x * sin_az], axis=1))
        both = dot(jnp.concatenate([high, low], axis=0), tilt_hi[...])
        return both[0:SD] + both[SD : 2 * SD] + dot(high, tilt_lo[...])

    def from_frame(x):
        high, low = split(x)
        both = dot_nt(jnp.concatenate([high, low], axis=0), tilt_hi[...])
        u = both[0:SD] + both[SD : 2 * SD] + dot_nt(high, tilt_lo[...])
        return (u[:, 0:CP] * cos_az + u[:, CP : 2 * CP] * sin_az) * root

    my_rows = pl.ds(pl.multiple_of(slot * SD, SD), SD)
    for h in range(2):
        v = jnp.concatenate([vec_ref[:, h, :], jnp.zeros((SD, CP - C), F32)], axis=1)
        vec[h] = v
        field[0, h, my_rows, :] = to_frame(v)

    pl.semaphore_wait(barrier, 2 * (LINE - 1) + NZ * NC - 1)

    def src_copy(i):
        peer = plane_peer(i // NC)
        peer = (peer[0], peer[1], mz, lax.rem(mc + lax.rem(i, NC), NC))
        return remote(geo_src_out, geo_src.at[slot], geo_src_send.at[i], geo_src_recv.at[i], peer)

    def tgt_copy(j):
        return remote(
            geo_tgt_out, geo_tgt.at[j], geo_tgt_send.at[j], geo_tgt_recv.at[j], line_peer(j)
        )

    def flag_copy(j):
        to = lax.rem(mz + j, NZ)
        return remote(
            flag_out.at[to], flag_in.at[j], flag_send.at[j], flag_recv.at[j], line_peer(j)
        )

    def field_copy(a, h, i):
        at = field.at[a, h, my_rows, :]
        return remote(at, at, field_send.at[a, h, i], field_recv.at[a, h, i], plane_peer(i))

    def pair_copy(a, h, i):
        rows = pl.ds(pl.multiple_of((plane_source(i) * NC + mc) * SD, SD), SD)
        at = field.at[a, h, rows, :]
        return remote(at, at, pair_send.at[a, h, i], pair_recv.at[a, h, i], partner)

    def part_copy(a, h, j):
        to = pl.ds(pl.multiple_of(lax.rem(mz + j, NZ) * SD, SD), SD)
        return remote(
            part.at[a, h, to, :], got.at[a, h, j], part_send.at[a, h, j], part_recv.at[a, h, j],
            line_peer(j),
        )

    def sa_copy(r, j):
        return remote(
            scal_out.at[r], scal_a.at[r, j], sa_send.at[r, j], sa_recv.at[r, j], pillar_peer(j)
        )

    def sb_copy(r, i):
        return remote(
            scal_mid.at[r], scal_b.at[r, i], sb_send.at[r, i], sb_recv.at[r, i], plane_peer(i)
        )

    def every(lo, hi, step):
        def body(k, carry):
            step(k)
            return carry

        lax.fori_loop(lo, hi, body, 0)

    def send_field(a, h):
        every(1, LINE, lambda i: field_copy(a, h, i).start())
        pair_copy(a, h, 0).start()

    every(1, LINE * NC, lambda i: src_copy(i).start())
    every(1, NZ, lambda j: tgt_copy(j).start())
    every(1, NZ, lambda j: flag_copy(j).start())
    send_field(0, 0)
    send_field(0, 1)

    ax_copy.wait()
    for m in range(TERMS):
        block = jnp.concatenate([axial[m], jnp.zeros((C, CP - C), F32)], axis=1)
        high, low = split(block)
        for ref, value in ((ax_hi, high), (ax_lo, low)):
            ref[m * CP : m * CP + C, :] = value
            ref[m * CP + C : (m + 1) * CP, :] = zeros_pad

    every(1, LINE * NC, lambda i: src_copy(i).wait_recv())
    every(1, NZ, lambda j: tgt_copy(j).wait_recv())
    src_rows = []
    for tile in range(SRC // 128):
        total = geo_src[8 * tile]
        for k in range(1, 8):
            total = total + geo_src[8 * tile + k]
        src_rows.append(total)
    src_all = jnp.concatenate(src_rows, axis=1)
    tgt_all = geo_tgt[0]
    for j in range(1, NZ):
        tgt_all = tgt_all + geo_tgt[j]
    mine[...] = tgt_all
    geo_cols = jnp.transpose(jnp.concatenate([tgt_all] * 16, axis=0))
    geo_col_ref = g_col = None
    del geo_col_ref, g_col
    part[0, 0, :, 0:128] = geo_cols

    def weigh(flags, z):
        rows = pl.ds(pl.multiple_of(z * SD, SD), SD)
        tgt = part[0, 0, rows, 0:128]
        dx = tgt[:, 0:1] - src_all[0:1, :]
        dy = tgt[:, 1:2] - src_all[1:2, :]
        dz = tgt[:, 2:3] - src_all[2:3, :]
        dist = jnp.sqrt(dx * dx + dy * dy + dz * dz)
        ratio = (tgt[:, 3:4] + src_all[3:4, :]) / jnp.maximum(dist, dist_floor)
        sin_d, cos_d = sincos(wavenum * dist)
        scale = jnp.where(flags != 0, coupling, 0.0)
        near = jnp.where(flags == 1, coupling, 0.0)
        for m in range(TERMS):
            if m > 0:
                near = near * ratio
                scale = near
            wave = cos_d * float(np.cos(phase_step * m)) - sin_d * float(np.sin(phase_step * m))
            high, low = split(wave * scale)
            at = pl.ds(pl.multiple_of(m * TGT + z * SD, SD), SD)
            w_hi[at, :] = high
            w_lo[at, :] = low

    weigh(flag_out[mz], mz)

    def weigh_from(j, carry):
        flag_copy(j).wait_recv()
        weigh(flag_in[j], lax.rem(mz + NZ - j, NZ))
        return carry

    lax.fori_loop(1, NZ, weigh_from, 0)

    def couple(a, h):
        def relay(i):
            field_copy(a, h, i).wait_recv()
            pair_copy(a, h, i).start()

        every(1, LINE, relay)
        every(0, LINE, lambda i: pair_copy(a, h, i).wait_recv())
        high, low = split(field[a, h])
        f_hi[...] = high
        f_lo[...] = low
        for block in range(2):
            at = slice(block * 512, (block + 1) * 512)
            g = dot(w_hi[at, :], f_hi[...]) + dot(w_hi[at, :], f_lo[...]) + dot(w_lo[at, :], f_hi[...])
            g_high, g_low = split(g)
            for k in range(4):
                m = block * 4 + k
                g_lhs[0:TGT, m * CP : (m + 1) * CP] = g_high[k * TGT : (k + 1) * TGT]
                g_lhs[TGT : 2 * TGT, m * CP : (m + 1) * CP] = g_low[k * TGT : (k + 1) * TGT]
        both = dot(g_lhs[...], ax_hi[...])
        part[a, h] = both[0:TGT] + both[TGT : 2 * TGT] + dot(g_lhs[0:TGT, :], ax_lo[...])
        every(1, NZ, lambda j: part_copy(a, h, j).start())

    def collect(a, h):
        total = part[a, h, pl.ds(pl.multiple_of(mz * SD, SD), SD), :]
        every(1, NZ, lambda j: part_copy(a, h, j).wait_recv())
        for j in range(1, NZ):
            total = total + got[a, h, j]
        return from_frame(total)

    def reduce_pillar(r):
        every(1, NZ * NC, lambda j: sa_copy(r, j).wait_recv())
        total = scal_out[r]
        for j in range(1, NZ * NC):
            total = total + scal_a[r, j]
        scal_mid[r] = total
        every(1, LINE, lambda i: sb_copy(r, i).start())

    def reduce_plane(r):
        every(1, LINE, lambda i: sb_copy(r, i).wait_recv())
        total = scal_mid[r]
        for i in range(1, LINE):
            total = total + scal_b[r, i]
        return jnp.sum(total, axis=1, keepdims=True)

    couple(0, 0)
    couple(0, 1)
    for h in range(2):
        image = vec[h] - collect(0, h)
        img[h] = image
        field[1, h, my_rows, :] = to_frame(image)
        send_field(1, h)

    scal_out[...] = jnp.zeros((2, 8, 128), F32)
    scal_out[0, 0:1, :] = lanes_of(vec[0] * vec[0] + vec[1] * vec[1])
    scal_out[0, 1:2, :] = lanes_of(vec[0] * img[0] + vec[1] * img[1])
    every(1, NZ * NC, lambda j: sa_copy(0, j).start())
    couple(1, 0)
    reduce_pillar(0)
    couple(1, 1)
    sums = reduce_plane(0)
    rho_start = sums[0:1, :]
    alpha = rho_start / sums[1:2, :]

    def inner(left, right):
        return lanes_of(left[0] * right[0] + left[1] * right[1])

    half_step = []
    half_image = []
    for h in range(2):
        image = img[h]
        second = image - collect(1, h)
        half_step.append(vec[h] - alpha * image)
        half_image.append(image - alpha * second)
    right = [vec[0], vec[1]]
    scal_out[1, 0:1, :] = inner(half_image, half_step)
    scal_out[1, 1:2, :] = inner(half_image, half_image)
    scal_out[1, 2:3, :] = inner(right, half_step)
    scal_out[1, 3:4, :] = inner(right, half_image)
    every(1, NZ * NC, lambda j: sa_copy(1, j).start())
    reduce_pillar(1)
    sums = reduce_plane(1)
    omega = sums[0:1, :] / sums[1:2, :]
    rho_next = sums[2:3, :] - omega * sums[3:4, :]
    beta = rho_next / rho_start * (alpha / omega)
    for h in range(2):
        res = half_step[h] - omega * half_image[h]
        sol_ref[:, h, :] = (alpha * right[h] + omega * half_step[h])[:, 0:C]
        res_ref[:, h, :] = res[:, 0:C]
        dir_ref[:, h, :] = (res + beta * (right[h] - omega * img[h]))[:, 0:C]

    every(1, LINE * NC, lambda i: src_copy(i).wait_send())
    every(1, NZ, lambda j: tgt_copy(j).wait_send())
    every(1, NZ, lambda j: flag_copy(j).wait_send())
    for a in range(2):
        for h in range(2):
            every(1, LINE, lambda i: field_copy(a, h, i).wait_send())
            every(0, LINE, lambda i: pair_copy(a, h, i).wait_send())
            every(1, NZ, lambda j: part_copy(a, h, j).wait_send())
        every(1, NZ * NC, lambda j: sa_copy(a, j).wait_send())
        every(1, LINE, lambda i: sb_copy(a, i).wait_send())


def on_device(
    right_side, positions, sphere_radii, azimuths, pair_flags, pair_counts, tilt_matrix, axial_terms
):
    vmem = pl.BlockSpec(memory_space=pltpu.VMEM)
    hbm = pl.BlockSpec(memory_space=pl.ANY)
    dma = pltpu.SemaphoreType.DMA
    out = jax.ShapeDtypeStruct((SD, 2, C), F32)
    V = pltpu.VMEM
    return tuple(
        pl.pallas_call(
            kernel,
            name="bicgstab",
            out_shape=(out, out, out),
            in_specs=[vmem] * 7 + [hbm, vmem],
            out_specs=(vmem, vmem, vmem),
            scratch_shapes=[
                V((TERMS, C, C), F32),
                V((TERMS * CP, CP), BF),
                V((TERMS * CP, CP), BF),
                V((2 * CP, CP), BF),
                V((2 * CP, CP), BF),
                V((NZ, SD, SRC), jnp.int32),
                V((NZ, SD, SRC), jnp.int32),
                V((8, 128), F32),
                V((8, 128), F32),
                V((8, 128), F32),
                V((LINE * NC, 8, 128), F32),
                V((NZ, 8, 128), F32),
                V((TERMS * TGT, SRC), BF),
                V((TERMS * TGT, SRC), BF),
                V((2, 2, SRC, CP), F32),
                V((SRC, CP), BF),
                V((SRC, CP), BF),
                V((2 * TGT, TERMS * CP), BF),
                V((2, 2, TGT, CP), F32),
                V((2, 2, NZ, SD, CP), F32),
                V((2, SD, CP), F32),
                V((2, SD, CP), F32),
                V((2, SD, CP), F32),
                V((2, 8, 128), F32),
                V((2, NZ * NC, 8, 128), F32),
                V((2, 8, 128), F32),
                V((2, LINE, 8, 128), F32),
                dma(()),
                dma((LINE * NC,)),
                dma((LINE * NC,)),
                dma((NZ,)),
                dma((NZ,)),
                dma((NZ,)),
                dma((NZ,)),
                dma((2, 2, LINE)),
                dma((2, 2, LINE)),
                dma((2, 2, LINE)),
                dma((2, 2, LINE)),
                dma((2, 2, NZ)),
                dma((2, 2, NZ)),
                dma((2, NZ * NC)),
                dma((2, NZ * NC)),
                dma((2, LINE)),
                dma((2, LINE)),
            ],
            compiler_params=pltpu.CompilerParams(
                collective_id=0, has_side_effects=True, vmem_limit_bytes=48 * 1024 * 1024
            ),
        )(
            right_side,
            positions,
            sphere_radii.reshape(1, SD),
            azimuths.reshape(1, SD),
            pair_flags,
            pair_counts.reshape(1, SD),
            tilt_matrix,
            axial_terms,
            jnp.asarray(orders_rows()),
        )
    )


def solution(mesh):
    split_mesh = Mesh(mesh.devices.reshape(NX, NY, NZ, NC), SPH)
    placed = (P(SPH, None, None), P(None, SPH), P(SPH), P(SPH), P(SPH, None), P(SPH), P(), P())
    return jax.shard_map(
        on_device,
        mesh=split_mesh,
        in_specs=placed,
        out_specs=(P(SPH, None, None), P(SPH, None, None), P(SPH, None, None)),
        check_vma=False,
    )
```

time: 350 us -> 87.6 us (0.25); the launches traced: 344 us -> 87.2 us
  blocking collectives: 138 us -> 0 us
  waiting for transfers between devices: 85.9 us -> 0 us
  Pallas kernels: 0 us -> 76.4 us
  matrix products: 46.4 us -> 0 us
  starting transfers between devices: 28.4 us -> 0 us
  other arithmetic: 16.4 us -> 0 us
  local copies, waits for them, and re-layouts: 20.3 us -> 10.2 us
  between operations: 8.58 us -> 0.66 us
    ppermute x20 -> x0, waiting for transfers between devices: 85.9 us -> none  [from_partner(): return lax.ppermute(value, axis, pairs)]
    psum x8 -> x0, blocking collectives: 82.7 us -> none  [by_axis(): x = lax.psum(x, axis)]
    pallas_call x0 -> x1, Pallas kernels: none -> 76.4 us  [on_device(): pl.pallas_call(kernel, name='bicgstab', out_shape=(out, out, out), in_spe...]
    all_gather x4 -> x0, blocking collectives: 55.1 us -> none  [stacked_from(): parts = lax.all_gather(parts, axes[k])]
    dot_general x8 -> x0, matrix products: 46.4 us -> none  [the longest x2 31.2 us: apply_op(): jnp.einsum('mtpk,mkl->tpl', gathered, axial_terms, precision=lax.Precisio...]
    ppermute x20 -> x0, starting transfers between devices: 28.4 us -> none  [from_partner(): return lax.ppermute(value, axis, pairs)]
    reshape x5 -> x0, local copies, waits for them, and re-layouts: 13.6 us -> none  [the longest x2 13.1 us: apply_op(): gathered = gathered.reshape(TERMS, group_width, 2, -1)]
    unnamed x8 -> x0, other arithmetic: 9.88 us -> none
  transfers between devices with their start and end apart: 20 -> 0, of which waited for: 14 -> 0; matrix products, arithmetic and copies ran while one was open for 5% -> 0% of each run, Pallas kernels for 0% -> 0%
where the time goes in v1:
time: 87.6 us; the launch traced here: 87.2 us
  Pallas kernels  76.4 us (87%)
  local copies, waits for them, and re-layouts  10.2 us (12%)
    pallas_call x1, Pallas kernels, on_device(): pl.pallas_call(kernel, name='bicgstab', out_shape=(out, out, out), in_spe...  76.4 us
    unnamed x21, local copies, waits for them, and re-layouts  10.2 us

profile of v1, /device:TPU:1, one launch (start us, length us, event | category | flops | bytes accessed | tf_op | source)
XLA Modules:
  0.0 87.2 jit_solution(1586652569016266180)
XLA Ops:
  0.6 0.0 copy-start
  0.6 2.2 %copy-done = f32[8,336,336]{2,1,0:T(8,128)S(1)} copy-done((f32[8,336,336]{2,1,0:T(8,128)S(1)}, f32[8,336,336]{2,1,0:T(8,128)}, u32[]{:S(2)}) %copy-start) | copy-done | bytes 3612696
  2.8 0.0 copy-start.1
  2.8 1.0 %copy-done.1 = f32[336,336]{1,0:T(8,128)S(1)} copy-done((f32[336,336]{1,0:T(8,128)S(1)}, f32[336,336]{1,0:T(8,128)}, u32[]{:S(2)}) %copy-start.1) | copy-done | bytes 451608
  3.8 0.0 copy-start.2
  3.8 0.9 %copy-done.2 = s32[16,4096]{1,0:T(8,128)S(1)} copy-done((s32[16,4096]{1,0:T(8,128)S(1)}, s32[16,4096]{1,0:T(8,128)}, u32[]{:S(2)}) %copy-start.2) | copy-done | bytes 262168
  4.8 0.0 copy-start.3
  4.8 0.8 copy-done.3
  5.6 0.0 copy-start.4
  5.6 0.7 copy-done.4
  6.3 0.0 copy-start.5
  6.3 0.7 copy-done.5
  7.0 0.0 copy-start.6
  7.0 0.7 copy-done.6
  7.6 0.0 copy-start.7
  7.6 0.7 copy-done.7
  8.3 0.0 copy-start.8
  8.3 0.7 copy-done.8
  8.9 76.4 %bicgstab.1 = (f32[16,2,336]{2,1,0:T(2,128)S(1)}, f32[16,2,336]{2,1,0:T(2,128)S(1)}, f32[16,2,336]{2,1,0:T(2,128)S(1)}) custom-call(f32[16,2,336]{2,1,0:T(2,128)S(1)} %copy-done.3, f32[3,16]{1,0:T(4,128)S(1)} %copy-done.5, f32[1,16]{1,0:T(1,128)S(1)} %bitcast.3, f32[1,16]{1,0:T(1,128)S(1)} %bitcast.4, s32[16,4096]{1,0:T(8,128)S(1)} %copy-done.2, ...), custom_call_target="tpu_custom_call" | custom-call | tf_op jit(solution)/shard_map/bicgstab/pallas_call | solution.py:428
  85.4 0.6 copy.15
  86.0 0.6 copy.16
  86.6 0.6 copy.17
Async XLA Ops:
  0.6 2.2 %copy-start = (f32[8,336,336]{2,1,0:T(8,128)S(1)}, f32[8,336,336]{2,1,0:T(8,128)}, u32[]{:S(2)}) copy-start(f32[8,336,336]{2,1,0:T(8,128)} %axial_hbm.1) | copy-start | bytes 10838020
  2.8 1.0 %copy-start.1 = (f32[336,336]{1,0:T(8,128)S(1)}, f32[336,336]{1,0:T(8,128)}, u32[]{:S(2)}) copy-start(f32[336,336]{1,0:T(8,128)} %tilt_ref.1) | copy-start | bytes 1354756
  3.8 0.9 %copy-start.2 = (s32[16,4096]{1,0:T(8,128)S(1)}, s32[16,4096]{1,0:T(8,128)}, u32[]{:S(2)}) copy-start(s32[16,4096]{1,0:T(8,128)} %flags_ref.1) | copy-start | bytes 786436
  4.8 0.8 copy-start.3
  5.6 0.7 copy-start.4
  6.3 0.7 copy-start.5
  7.0 0.7 copy-start.6
  7.6 0.7 copy-start.7
  8.3 0.7 copy-start.8

commit v2 on v1

v2 whole, which is shorter than its diff:
```python
import functools

import jax
import jax.numpy as jnp
import numpy as np
from jax import lax
from jax.experimental import pallas as pl
from jax.experimental.pallas import tpu as pltpu
from jax.sharding import Mesh
from jax.sharding import PartitionSpec as P

DEG = 12
TERMS = 8
SPH = ("sph_0", "sph_1", "sph_2", "sph_3")
NX, NY, NZ, NC = 4, 4, 8, 2
MESH = pl.DeviceIdType.MESH

coupling = 0.25
wavenum = 2.5
phase_step = 0.9
dist_floor = 0.8

SD = 16
HALF = 168
C = 336
CP = 384
LINE = NX * NY
SRC = LINE * NC * SD
TGT = NZ * SD
RINGS = (
    ((2, 2), (1, 2), (3, 2), (2, 1), (2, 3)),
    ((0, 2), (2, 0), (1, 1), (1, 3), (3, 1), (3, 3)),
    ((0, 1), (0, 3), (1, 0), (3, 0)),
)
LINE_ORDER = (4, 3, 5, 2, 6, 1, 7)
PLANE_ORDER = tuple(offset for ring in RINGS for offset in ring)
PILLAR_ORDER = tuple((j, core) for j in LINE_ORDER for core in (1, 0)) + ((0, 1),)
BF = jnp.bfloat16
F32 = jnp.float32


def orders_rows():
    orders = np.concatenate([np.arange(-degree, degree + 1) for degree in range(1, DEG + 1)])
    rows = np.zeros((8, CP), np.float32)
    rows[0, :HALF] = orders
    rows[0, HALF:C] = orders
    rows[1, :HALF] = 1.0
    rows[1, HALF:C] = -1.0
    return rows


def sincos(x):
    q = jnp.floor(x * (2.0 / np.pi) + 0.5)
    r = x - q * 1.5703125
    r = r - q * 4.83751296997070312e-4
    r = r - q * 7.54978995489188216e-8
    r2 = r * r
    s = r + r * r2 * (-1.6666654611e-1 + r2 * (8.3321608736e-3 + r2 * (-1.9515295891e-4)))
    c = 1.0 - 0.5 * r2 + r2 * r2 * (
        4.166664568298827e-2 + r2 * (-1.388731625493765e-3 + r2 * 2.443315711809948e-5)
    )
    quad = q - 4.0 * jnp.floor(q * 0.25)
    odd = (quad == 1.0) | (quad == 3.0)
    sin_sign = jnp.where(quad >= 2.0, -1.0, 1.0)
    cos_sign = jnp.where((quad == 1.0) | (quad == 2.0), -1.0, 1.0)
    return jnp.where(odd, c, s) * sin_sign, jnp.where(odd, s, c) * cos_sign


def split(x):
    high = x.astype(BF)
    return high, (x - high.astype(F32)).astype(BF)


def dot(a, b):
    return lax.dot_general(a, b, (((1,), (0,)), ((), ())), preferred_element_type=F32)


def dot_nt(a, b):
    return lax.dot_general(a, b, (((1,), (1,)), ((), ())), preferred_element_type=F32)


def lanes_of(x):
    total = jnp.sum(x, axis=0, keepdims=True)
    return total[:, 0:128] + total[:, 128:256] + total[:, 256:384]


def kernel(
    vec_hbm, pos_hbm, rad_hbm, az_hbm, flags_hbm, counts_hbm, tilt_hbm, axial_hbm, rows_hbm,
    sol_ref, res_ref, dir_ref,
    vec_ref, pos_ref, rad_ref, az_ref, flags_ref, counts_ref, tilt_ref, axial, rows_ref, ax_hi, ax_lo, tilt_hi, tilt_lo, flag_out, flag_in, mine, geo_src_out, geo_tgt_out,
    geo_src, geo_tgt, w_hi, w_lo, field, f_hi, f_lo, g_lhs, part, got, vec, img, img2,
    scal_out, scal_a, scal_mid, scal_b,
    in_sem, geo_src_send, geo_src_recv, geo_tgt_send, geo_tgt_recv, flag_send, flag_recv,
    field_send, field_recv, pair_send, pair_recv, part_send, part_recv,
    sa_send, sa_recv, sb_send, sb_recv,
):
    mx, my, mz, mc = (lax.axis_index(name) for name in SPH)
    plane = mx * NY + my
    slot = plane * NC + mc

    def plane_peer(offset, core):
        return (lax.rem(mx + offset[0], NX), lax.rem(my + offset[1], NY), mz, core)

    def line_peer(j):
        return (mx, my, lax.rem(mz + j, NZ), mc)

    def pillar_peer(j, core):
        return (mx, my, lax.rem(mz + j, NZ), mc if core == 0 else 1 - mc)

    partner = (mx, my, mz, 1 - mc)

    def remote(src, dst, send, recv, peer):
        return pltpu.make_async_remote_copy(
            src_ref=src, dst_ref=dst, send_sem=send, recv_sem=recv, device_id=peer,
            device_id_type=MESH,
        )

    with jax.named_scope("loads"):
        pairs = (
            (pos_hbm, pos_ref), (rad_hbm, rad_ref), (az_hbm, az_ref), (counts_hbm, counts_ref),
            (rows_hbm, rows_ref), (flags_hbm, flags_ref), (tilt_hbm, tilt_ref), (vec_hbm, vec_ref),
            (axial_hbm, axial),
        )
        loads = [pltpu.make_async_copy(a, b, in_sem.at[k]) for k, (a, b) in enumerate(pairs)]
        for load in loads:
            load.start()

        barrier = pltpu.get_barrier_semaphore()

        def greet(peer):
            pl.semaphore_signal(barrier, inc=1, device_id=peer, device_id_type=MESH)

        for j, core in PILLAR_ORDER:
            greet(pillar_peer(j, core))
        for offset in PLANE_ORDER:
            for core in range(NC):
                greet(plane_peer(offset, core))

        for load in loads[:6]:
            load.wait()

    with jax.named_scope("geo_prep"):
        mine[...] = jnp.zeros((8, 128), F32)
        mine[0:3, 0:SD] = pos_ref[...]
        mine[3:4, 0:SD] = rad_ref[...]
        mine[4:5, 0:SD] = az_ref[...]
        mine[5:6, 0:SD] = counts_ref[...].astype(F32)
        own = mine[...]
        lane = lax.broadcasted_iota(jnp.int32, (8, 128), 1)
        spread = own
        for shift in (16, 32, 64):
            spread = spread + pltpu.roll(spread, shift, 1)
        geo_src_out[...] = jnp.where(lane // SD == lax.rem(slot, 8), spread, 0.0)
        geo_tgt_out[...] = jnp.where(lane // SD == mz, spread, 0.0)
        geo_src[pl.ds(slot, 1)] = geo_src_out[...][None]
        geo_tgt[pl.ds(0, 1)] = geo_tgt_out[...][None]

    with jax.named_scope("flag_prep"):
        for z in range(NZ):
            r = z % 4
            for j in range(4):
                tile = None
                for i in range(4):
                    at = ((4 * j + i) * 2 + z // 4) * 128
                    piece = flags_ref[:, at : at + 128]
                    if i != r:
                        piece = pltpu.roll(piece, (32 * (i - r)) % 128, 1)
                    if tile is None:
                        tile = piece
                    else:
                        where = lax.broadcasted_iota(jnp.int32, (SD, 128), 1) // 32 == i
                        tile = jnp.where(where, piece, tile)
                flag_out[z, :, 128 * j : 128 * (j + 1)] = tile

    loads[6].wait()
    loads[7].wait()
    cols = jnp.transpose(jnp.concatenate([own] * 16, axis=0))
    azimuth = cols[0:SD, 4:5]
    root = 1.0 / jnp.sqrt(1.0 + cols[0:SD, 5:6])
    sin_az, cos_az = sincos(azimuth * rows_ref[0:1, :])
    sin_az = sin_az * rows_ref[1:2, :]
    zeros_pad = jnp.zeros((CP - C, CP), BF)
    for half in range(2):
        for which, ref in enumerate((tilt_hi, tilt_lo)):
            ref[half * CP + C : half * CP + CP, :] = zeros_pad
    for half, (a, b) in enumerate(((0, HALF), (HALF, 0))):
        block = jnp.concatenate(
            [tilt_ref[a : a + HALF, :], tilt_ref[b : b + HALF, :]], axis=0
        )
        block = jnp.concatenate([block, jnp.zeros((C, CP - C), F32)], axis=1)
        high, low = split(block)
        tilt_hi[half * CP : half * CP + C, :] = high
        tilt_lo[half * CP : half * CP + C, :] = low

    def to_frame(x):
        high, low = split(jnp.concatenate([x * cos_az, x * sin_az], axis=1))
        both = dot(jnp.concatenate([high, low], axis=0), tilt_hi[...])
        return both[0:SD] + both[SD : 2 * SD] + dot(high, tilt_lo[...])

    def from_frame(x):
        high, low = split(x)
        both = dot_nt(jnp.concatenate([high, low], axis=0), tilt_hi[...])
        u = both[0:SD] + both[SD : 2 * SD] + dot_nt(high, tilt_lo[...])
        return (u[:, 0:CP] * cos_az + u[:, CP : 2 * CP] * sin_az) * root

    my_rows = pl.ds(pl.multiple_of(slot * SD, SD), SD)
    with jax.named_scope("frame0"):
        for h in range(2):
            v = jnp.concatenate([vec_ref[:, h, :], jnp.zeros((SD, CP - C), F32)], axis=1)
            vec[h] = v
            field[0, h, my_rows, :] = to_frame(v)

    with jax.named_scope("barrier_wait"):
        pl.semaphore_wait(barrier, 2 * (LINE - 1) + NZ * NC - 1)

    def src_copy(peer):
        return remote(geo_src_out, geo_src.at[slot], geo_src_send, geo_src_recv, peer)

    src_all_copies = remote(
        geo_src.at[pl.ds(0, LINE * NC - 1)], geo_src.at[pl.ds(0, LINE * NC - 1)],
        geo_src_send, geo_src_recv, partner,
    )

    def tgt_copy(j):
        return remote(geo_tgt_out, geo_tgt.at[j], geo_tgt_send, geo_tgt_recv, line_peer(j))

    tgt_all_copies = remote(
        geo_tgt.at[pl.ds(0, NZ - 1)], geo_tgt.at[pl.ds(0, NZ - 1)],
        geo_tgt_send, geo_tgt_recv, partner,
    )

    def flag_copy(j):
        to = lax.rem(mz + j, NZ)
        return remote(flag_out.at[to], flag_in.at[j], flag_send, flag_recv.at[j], line_peer(j))

    def blocks(a, h, count, send, recv):
        at = field.at[a, h, pl.ds(0, count * SD), :]
        return remote(at, at, send, recv, partner)

    def field_copy(a, h, ring, offset):
        at = field.at[a, h, my_rows, :]
        return remote(
            at, at, field_send.at[a, h], field_recv.at[a, h, ring], plane_peer(offset, 1 - mc)
        )

    def pair_copy(a, h, offset):
        source = lax.rem(mx + NX - offset[0], NX) * NY + lax.rem(my + NY - offset[1], NY)
        core = mc if offset == (0, 0) else 1 - mc
        rows = pl.ds(pl.multiple_of((source * NC + core) * SD, SD), SD)
        at = field.at[a, h, rows, :]
        return remote(at, at, pair_send.at[a, h], pair_recv.at[a, h], partner)

    def send_part(a, h):
        for k, j in enumerate(LINE_ORDER):
            to = pl.ds(pl.multiple_of(lax.rem(mz + j, NZ) * SD, SD), SD)
            remote(
                part.at[a, h, to, :], got.at[a, h, k], part_send.at[a, h], part_recv.at[a, h],
                line_peer(j),
            ).start()

    def part_all(a, h):
        at = got.at[a, h, pl.ds(0, NZ - 1)]
        return remote(at, at, part_send.at[a, h], part_recv.at[a, h], partner)

    def send_pillar(r):
        for k, (j, core) in enumerate(PILLAR_ORDER):
            remote(
                scal_out.at[r], scal_a.at[r, k], sa_send.at[r], sa_recv.at[r], pillar_peer(j, core)
            ).start()

    def sa_all(r):
        at = scal_a.at[r, pl.ds(0, NZ * NC - 1)]
        return remote(at, at, sa_send.at[r], sa_recv.at[r], partner)

    def send_plane(r):
        for k, offset in enumerate(PLANE_ORDER):
            remote(
                scal_mid.at[r], scal_b.at[r, k], sb_send.at[r], sb_recv.at[r],
                plane_peer(offset, mc),
            ).start()

    def sb_all(r):
        at = scal_b.at[r, pl.ds(0, LINE - 1)]
        return remote(at, at, sb_send.at[r], sb_recv.at[r], partner)

    def send_field(a, h):
        for ring, offsets in enumerate(RINGS):
            for offset in offsets:
                field_copy(a, h, ring, offset).start()
        pair_copy(a, h, (0, 0)).start()

    def relay(a, h, ring):
        with jax.named_scope(f"relay{a}{h}{ring}"):
            blocks(a, h, len(RINGS[ring]), field_send.at[a, h], field_recv.at[a, h, ring]).wait_recv()
            for offset in RINGS[ring]:
                pair_copy(a, h, offset).start()

    with jax.named_scope("sends"):
        for offset in PLANE_ORDER:
            for core in range(NC):
                src_copy(plane_peer(offset, core)).start()
        src_copy(partner).start()
        for j in LINE_ORDER:
            tgt_copy(j).start()
        for j in LINE_ORDER:
            flag_copy(j).start()
        send_field(0, 0)
        send_field(0, 1)

    with jax.named_scope("axial"):
        loads[8].wait()
        for m in range(TERMS):
            block = jnp.concatenate([axial[m], jnp.zeros((C, CP - C), F32)], axis=1)
            high, low = split(block)
            for ref, value in ((ax_hi, high), (ax_lo, low)):
                ref[m * CP : m * CP + C, :] = value
                ref[m * CP + C : (m + 1) * CP, :] = zeros_pad

    with jax.named_scope("geo_wait"):
        src_all_copies.wait_recv()
        tgt_all_copies.wait_recv()
    src_rows = []
    for tile in range(SRC // 128):
        total = geo_src[8 * tile]
        for k in range(1, 8):
            total = total + geo_src[8 * tile + k]
        src_rows.append(total)
    src_all = jnp.concatenate(src_rows, axis=1)
    tgt_all = geo_tgt[0]
    for j in range(1, NZ):
        tgt_all = tgt_all + geo_tgt[j]
    part[0, 0, :, 0:128] = jnp.transpose(jnp.concatenate([tgt_all] * 16, axis=0))

    def weigh(flags, z):
        rows = pl.ds(pl.multiple_of(z * SD, SD), SD)
        tgt = part[0, 0, rows, 0:128]
        dx = tgt[:, 0:1] - src_all[0:1, :]
        dy = tgt[:, 1:2] - src_all[1:2, :]
        dz = tgt[:, 2:3] - src_all[2:3, :]
        dist = jnp.sqrt(dx * dx + dy * dy + dz * dz)
        ratio = (tgt[:, 3:4] + src_all[3:4, :]) / jnp.maximum(dist, dist_floor)
        sin_d, cos_d = sincos(wavenum * dist)
        scale = jnp.where(flags != 0, coupling, 0.0)
        near = jnp.where(flags == 1, coupling, 0.0)
        for m in range(TERMS):
            if m > 0:
                near = near * ratio
                scale = near
            wave = cos_d * float(np.cos(phase_step * m)) - sin_d * float(np.sin(phase_step * m))
            high, low = split(wave * scale)
            at = pl.ds(pl.multiple_of(m * TGT + z * SD, SD), SD)
            w_hi[at, :] = high
            w_lo[at, :] = low

    with jax.named_scope("weigh"):
        weigh(flag_out[mz], mz)

        def weigh_from(j, carry):
            flag_copy(j).wait_recv()
            weigh(flag_in[j], lax.rem(mz + NZ - j, NZ))
            return carry

        for ring, (lo, hi) in enumerate(((1, 5), (5, 7), (7, 8))):
            lax.fori_loop(lo, hi, weigh_from, 0)
            relay(0, 0, ring)

    def couple(a, h):
        with jax.named_scope(f"gather_wait{a}{h}"):
            blocks(a, h, LINE, pair_send.at[a, h], pair_recv.at[a, h]).wait_recv()
        with jax.named_scope(f"first{a}{h}"):
            high, low = split(field[a, h])
            f_hi[...] = high
            f_lo[...] = low
            for block in range(2):
                at = slice(block * 512, (block + 1) * 512)
                g = dot(w_hi[at, :], f_hi[...]) + dot(w_hi[at, :], f_lo[...]) + dot(w_lo[at, :], f_hi[...])
                g_high, g_low = split(g)
                for k in range(4):
                    m = block * 4 + k
                    g_lhs[0:TGT, m * CP : (m + 1) * CP] = g_high[k * TGT : (k + 1) * TGT]
                    g_lhs[TGT : 2 * TGT, m * CP : (m + 1) * CP] = g_low[k * TGT : (k + 1) * TGT]
        if h == 0:
            for ring in range(len(RINGS)):
                relay(a, 1, ring)
        with jax.named_scope(f"second{a}{h}"):
            both = dot(g_lhs[...], ax_hi[...])
            part[a, h] = both[0:TGT] + both[TGT : 2 * TGT] + dot(g_lhs[0:TGT, :], ax_lo[...])
            send_part(a, h)

    def collect(a, h):
        total = part[a, h, pl.ds(pl.multiple_of(mz * SD, SD), SD), :]
        with jax.named_scope(f"part_wait{a}{h}"):
            part_all(a, h).wait_recv()
        for k in range(NZ - 1):
            total = total + got[a, h, k]
        return from_frame(total)

    def reduce_pillar(r):
        with jax.named_scope(f"pillar_wait{r}"):
            sa_all(r).wait_recv()
        total = scal_out[r]
        for k in range(NZ * NC - 1):
            total = total + scal_a[r, k]
        scal_mid[r] = total
        send_plane(r)

    def reduce_plane(r):
        with jax.named_scope(f"plane_wait{r}"):
            sb_all(r).wait_recv()
        total = scal_mid[r]
        for k in range(LINE - 1):
            total = total + scal_b[r, k]
        return jnp.sum(total, axis=1, keepdims=True)

    couple(0, 0)
    couple(0, 1)
    for h in range(2):
        image = vec[h] - collect(0, h)
        img[h] = image
        field[1, h, my_rows, :] = to_frame(image)
        send_field(1, h)

    scal_out[...] = jnp.zeros((2, 8, 128), F32)
    scal_out[0, 0:1, :] = lanes_of(vec[0] * vec[0] + vec[1] * vec[1])
    scal_out[0, 1:2, :] = lanes_of(vec[0] * img[0] + vec[1] * img[1])
    send_pillar(0)
    for ring in range(len(RINGS)):
        relay(1, 0, ring)
    couple(1, 0)
    reduce_pillar(0)
    couple(1, 1)
    sums = reduce_plane(0)
    rho_start = sums[0:1, :]
    alpha = rho_start / sums[1:2, :]

    def inner(left, right):
        return lanes_of(left[0] * right[0] + left[1] * right[1])

    half_step = []
    half_image = []
    for h in range(2):
        image = img[h]
        second = image - collect(1, h)
        half_step.append(vec[h] - alpha * image)
        half_image.append(image - alpha * second)
    right = [vec[0], vec[1]]
    scal_out[1, 0:1, :] = inner(half_image, half_step)
    scal_out[1, 1:2, :] = inner(half_image, half_image)
    scal_out[1, 2:3, :] = inner(right, half_step)
    scal_out[1, 3:4, :] = inner(right, half_image)
    send_pillar(1)
    reduce_pillar(1)
    sums = reduce_plane(1)
    omega = sums[0:1, :] / sums[1:2, :]
    rho_next = sums[2:3, :] - omega * sums[3:4, :]
    beta = rho_next / rho_start * (alpha / omega)
    for h in range(2):
        res = half_step[h] - omega * half_image[h]
        sol_ref[:, h, :] = (alpha * right[h] + omega * half_step[h])[:, 0:C]
        res_ref[:, h, :] = res[:, 0:C]
        dir_ref[:, h, :] = (res + beta * (right[h] - omega * img[h]))[:, 0:C]

    with jax.named_scope("drain"):
        src_all_copies.wait_send()
        tgt_all_copies.wait_send()
        sent = flag_in.at[pl.ds(0, NZ - 1)]
        remote(sent, sent, flag_send, flag_recv.at[0], partner).wait_send()
        for a in range(2):
            for h in range(2):
                blocks(a, h, LINE - 1, field_send.at[a, h], field_recv.at[a, h, 0]).wait_send()
                blocks(a, h, LINE, pair_send.at[a, h], pair_recv.at[a, h]).wait_send()
                part_all(a, h).wait_send()
            sa_all(a).wait_send()
            sb_all(a).wait_send()


def put_out(*refs):
    for k in range(3):
        refs[3 + k][...] = refs[k][...]


def on_device(
    right_side, positions, sphere_radii, azimuths, pair_flags, pair_counts, tilt_matrix, axial_terms
):
    vmem = pl.BlockSpec(memory_space=pltpu.VMEM)
    hbm = pl.BlockSpec(memory_space=pltpu.HBM)
    dma = pltpu.SemaphoreType.DMA
    out = jax.ShapeDtypeStruct((SD, 2, C), F32)
    V = pltpu.VMEM
    results = tuple(
        pl.pallas_call(
            kernel,
            name="bicgstab",
            out_shape=(out, out, out),
            in_specs=[hbm] * 9,
            out_specs=(vmem, vmem, vmem),
            scratch_shapes=[
                V((SD, 2, C), F32),
                V((3, SD), F32),
                V((1, SD), F32),
                V((1, SD), F32),
                V((SD, LINE * NZ * NC * SD), jnp.int32),
                V((1, SD), jnp.int32),
                V((C, C), F32),
                V((TERMS, C, C), F32),
                V((8, CP), F32),
                V((TERMS * CP, CP), BF),
                V((TERMS * CP, CP), BF),
                V((2 * CP, CP), BF),
                V((2 * CP, CP), BF),
                V((NZ, SD, SRC), jnp.int32),
                V((NZ, SD, SRC), jnp.int32),
                V((8, 128), F32),
                V((8, 128), F32),
                V((8, 128), F32),
                V((LINE * NC, 8, 128), F32),
                V((NZ, 8, 128), F32),
                V((TERMS * TGT, SRC), BF),
                V((TERMS * TGT, SRC), BF),
                V((2, 2, SRC, CP), F32),
                V((SRC, CP), BF),
                V((SRC, CP), BF),
                V((2 * TGT, TERMS * CP), BF),
                V((2, 2, TGT, CP), F32),
                V((2, 2, NZ, SD, CP), F32),
                V((2, SD, CP), F32),
                V((2, SD, CP), F32),
                V((2, SD, CP), F32),
                V((2, 8, 128), F32),
                V((2, NZ * NC, 8, 128), F32),
                V((2, 8, 128), F32),
                V((2, LINE, 8, 128), F32),
                dma((9,)),
                dma(()),
                dma(()),
                dma(()),
                dma(()),
                dma(()),
                dma((NZ,)),
                dma((2, 2)),
                dma((2, 2, len(RINGS))),
                dma((2, 2)),
                dma((2, 2)),
                dma((2, 2)),
                dma((2, 2)),
                dma((2,)),
                dma((2,)),
                dma((2,)),
                dma((2,)),
            ],
            compiler_params=pltpu.CompilerParams(
                collective_id=0, has_side_effects=True
            ),
        )(
            right_side,
            positions,
            sphere_radii.reshape(1, SD),
            azimuths.reshape(1, SD),
            pair_flags,
            pair_counts.reshape(1, SD),
            tilt_matrix,
            axial_terms,
            jnp.asarray(orders_rows()),
        )
    )
    return tuple(
        pl.pallas_call(
            put_out,
            name="put_out",
            out_shape=(out, out, out),
            in_specs=[vmem] * 3,
            out_specs=(vmem,) * 3,
        )(*results)
    )


def solution(mesh):
    split_mesh = Mesh(mesh.devices.reshape(NX, NY, NZ, NC), SPH)
    placed = (P(SPH, None, None), P(None, SPH), P(SPH), P(SPH), P(SPH, None), P(SPH), P(), P())
    return jax.shard_map(
        on_device,
        mesh=split_mesh,
        in_specs=placed,
        out_specs=(P(SPH, None, None), P(SPH, None, None), P(SPH, None, None)),
        check_vma=False,
    )
```

time: 87.6 us -> 69.9 us (0.80)
  local copies, waits for them, and re-layouts: 10.2 us -> 0 us
  Pallas kernels: 76.4 us -> 69.1 us
    unnamed x21 -> x0, local copies, waits for them, and re-layouts: 10.2 us -> none
    pallas_call x1, Pallas kernels: 76.4 us -> 67.6 us  [on_device(): pl.pallas_call(kernel, name='bicgstab', out_shape=(out, out, out), in_spe...]
    pallas_call x0 -> x1, Pallas kernels: none -> 1.52 us  [on_device(): pl.pallas_call(put_out, name='put_out', out_shape=(out, out, out), in_spe...]
where the time goes in v2:
time: 69.9 us; the launch traced here: 69.7 us
  Pallas kernels  69.1 us (99%)
    pallas_call x1, Pallas kernels, on_device(): pl.pallas_call(kernel, name='bicgstab', out_shape=(out, out, out), in_spe...  67.6 us
    pallas_call x1, Pallas kernels, on_device(): pl.pallas_call(put_out, name='put_out', out_shape=(out, out, out), in_spe...  1.52 us

profile of v2, /device:TPU:1, one launch (start us, length us, event | category | flops | bytes accessed | tf_op | source)
XLA Modules:
  0.0 69.7 jit_solution(15169997218113119477)
XLA Ops:
  0.6 67.6 %bicgstab.1 = (f32[16,2,336]{2,1,0:T(2,128)}, f32[16,2,336]{2,1,0:T(2,128)}, f32[16,2,336]{2,1,0:T(2,128)}) custom-call(f32[16,2,336]{2,1,0:T(2,128)} %vec_hbm.1, f32[3,16]{1,0:T(4,128)} %pos_hbm.1, f32[1,16]{1,0:T(1,128)} %bitcast.3, f32[1,16]{1,0:T(1,128)} %bitcast.4, s32[16,4096]{1,0:T(8,128)} %flags_hbm.1, s32[1,16]{1,0:T(1,128)} %bitcast.5, ...), custom_call_target="tpu_custom_call" | custom-call | tf_op jit(solution)/shard_map/bicgstab/pallas_call | solution.py:491
  68.2 1.5 %put_out.1 = (f32[16,2,336]{2,1,0:T(2,128)}, f32[16,2,336]{2,1,0:T(2,128)}, f32[16,2,336]{2,1,0:T(2,128)}) custom-call(f32[16,2,336]{2,1,0:T(2,128)} %get-tuple-element.6.refs_0_, f32[16,2,336]{2,1,0:T(2,128)} %get-tuple-element.7.refs_1_, f32[16,2,336]{2,1,0:T(2,128)} %get-tuple-element.8.refs_2_), custom_call_target="tpu_custom_call" | custom-call | tf_op jit(solution)/shard_map/put_out/pallas_call | solution.py:567

commit v3 on v2

--- a/solution.py
+++ b/solution.py
@@ -25,6 +25,7 @@
 C = 336
 CP = 384
 LINE = NX * NY
+PACKED = 42
 SRC = LINE * NC * SD
 TGT = NZ * SD
 RINGS = (
@@ -75,8 +76,42 @@
     return lax.dot_general(a, b, (((1,), (0,)), ((), ())), preferred_element_type=F32)
 
 
-def dot_nt(a, b):
-    return lax.dot_general(a, b, (((1,), (1,)), ((), ())), preferred_element_type=F32)
+def spots():
+    lane = lax.broadcasted_iota(jnp.int32, (8, 128), 1)
+    row = lax.broadcasted_iota(jnp.int32, (8, 128), 0)
+    return lane, row % 4
+
+
+def pack(put, x):
+    lane, phase = spots()
+    for k in range(4):
+        at = slice(8 * (k % 2), 8 * (k % 2) + 8)
+        put(8 * k, x[at, 128 * (k // 2) : 128 * (k // 2) + 128])
+    upper, lower = x[0:8, 256:384], x[8:16, 256:384]
+    put(32, jnp.where(lane < 80, upper, pltpu.roll(lower, 80, 1)))
+    rest = jnp.zeros((8, 128), F32)
+    for p in range(4):
+        rest = jnp.where((phase == p) & (lane // 32 == p), pltpu.roll(lower, (32 * p + 80) % 128, 1), rest)
+    put(40, jnp.concatenate([jnp.sum(rest[4 * q : 4 * q + 4], axis=0, keepdims=True) for q in range(2)], axis=0))
+
+
+def unpack(tiles, tail):
+    lane, phase = spots()
+    both = tiles[4]
+    upper = jnp.where(lane < 80, both, 0.0)
+    wide = jnp.concatenate([jnp.broadcast_to(tail[q : q + 1], (4, 128)) for q in range(2)], axis=0)
+    rest = jnp.zeros((8, 128), F32)
+    for p in range(4):
+        rest = jnp.where(phase == p, pltpu.roll(wide, (48 - 32 * p) % 128, 1), rest)
+    lower = jnp.where(lane < 48, pltpu.roll(both, 48, 1), jnp.where(lane < 80, rest, 0.0))
+    return jnp.concatenate(
+        [
+            jnp.concatenate([tiles[0], tiles[1]], axis=0),
+            jnp.concatenate([tiles[2], tiles[3]], axis=0),
+            jnp.concatenate([upper, lower], axis=0),
+        ],
+        axis=1,
+    )
 
 
 def lanes_of(x):
@@ -87,8 +122,8 @@
 def kernel(
     vec_hbm, pos_hbm, rad_hbm, az_hbm, flags_hbm, counts_hbm, tilt_hbm, axial_hbm, rows_hbm,
     sol_ref, res_ref, dir_ref,
-    vec_ref, pos_ref, rad_ref, az_ref, flags_ref, counts_ref, tilt_ref, axial, rows_ref, ax_hi, ax_lo, tilt_hi, tilt_lo, flag_out, flag_in, mine, geo_src_out, geo_tgt_out,
-    geo_src, geo_tgt, w_hi, w_lo, field, f_hi, f_lo, g_lhs, part, got, vec, img, img2,
+    vec_ref, pos_ref, rad_ref, az_ref, flags_ref, counts_ref, tilt_ref, axial, rows_ref, ax_cat, tilt_in, tilt_out, flag_out, flag_in, mine, geo_src_out, geo_tgt_out,
+    geo_src, geo_tgt, w_cat, field, f_cat, g_lhs, g_acc, part, part_out, got, vec, img, img2,
     scal_out, scal_a, scal_mid, scal_b,
     in_sem, geo_src_send, geo_src_recv, geo_tgt_send, geo_tgt_recv, flag_send, flag_recv,
     field_send, field_recv, pair_send, pair_recv, part_send, part_recv,
@@ -96,7 +131,6 @@
 ):
     mx, my, mz, mc = (lax.axis_index(name) for name in SPH)
     plane = mx * NY + my
-    slot = plane * NC + mc
 
     def plane_peer(offset, core):
         return (lax.rem(mx + offset[0], NX), lax.rem(my + offset[1], NY), mz, core)
@@ -150,27 +184,32 @@
         spread = own
         for shift in (16, 32, 64):
             spread = spread + pltpu.roll(spread, shift, 1)
-        geo_src_out[...] = jnp.where(lane // SD == lax.rem(slot, 8), spread, 0.0)
+        geo_src_out[...] = jnp.where(lane // SD == lax.rem(plane, 8), spread, 0.0)
         geo_tgt_out[...] = jnp.where(lane // SD == mz, spread, 0.0)
-        geo_src[pl.ds(slot, 1)] = geo_src_out[...][None]
+        geo_src[pl.ds(plane, 1)] = geo_src_out[...][None]
         geo_tgt[pl.ds(0, 1)] = geo_tgt_out[...][None]
 
     with jax.named_scope("flag_prep"):
-        for z in range(NZ):
-            r = z % 4
-            for j in range(4):
-                tile = None
-                for i in range(4):
-                    at = ((4 * j + i) * 2 + z // 4) * 128
-                    piece = flags_ref[:, at : at + 128]
-                    if i != r:
-                        piece = pltpu.roll(piece, (32 * (i - r)) % 128, 1)
-                    if tile is None:
-                        tile = piece
-                    else:
-                        where = lax.broadcasted_iota(jnp.int32, (SD, 128), 1) // 32 == i
-                        tile = jnp.where(where, piece, tile)
-                flag_out[z, :, 128 * j : 128 * (j + 1)] = tile
+        lane = lax.broadcasted_iota(jnp.int32, (SD, 128), 1)
+        for upper in range(2):
+            for eight in range(2):
+                sides = ([], [])
+                for k in range(4):
+                    at = ((8 * eight + 2 * k) * 2 + upper) * 128
+                    first, second = flags_ref[:, at : at + 128], flags_ref[:, at + 256 : at + 384]
+                    even = jnp.where(lane % 32 < 16, first, pltpu.roll(second, 16, 1))
+                    odd = jnp.where(lane % 32 < 16, pltpu.roll(first, 112, 1), second)
+                    sides[0].append(jnp.where(mc == 0, even, odd))
+                    sides[1].append(jnp.where(mc == 0, odd, even))
+                for side in range(2):
+                    for r in range(4):
+                        tile = sides[side][r]
+                        for k in range(4):
+                            if k != r:
+                                piece = pltpu.roll(sides[side][k], (32 * (k - r)) % 128, 1)
+                                tile = jnp.where(lane // 32 == k, piece, tile)
+                        at = 128 * (2 * side + eight)
+                        flag_out[4 * upper + r, :, at : at + 128] = tile
 
     loads[6].wait()
     loads[7].wait()
@@ -180,41 +219,43 @@
     sin_az, cos_az = sincos(azimuth * rows_ref[0:1, :])
     sin_az = sin_az * rows_ref[1:2, :]
     zeros_pad = jnp.zeros((CP - C, CP), BF)
-    for half in range(2):
-        for which, ref in enumerate((tilt_hi, tilt_lo)):
-            ref[half * CP + C : half * CP + CP, :] = zeros_pad
-    for half, (a, b) in enumerate(((0, HALF), (HALF, 0))):
-        block = jnp.concatenate(
-            [tilt_ref[a : a + HALF, :], tilt_ref[b : b + HALF, :]], axis=0
-        )
+    turned = jnp.concatenate([tilt_ref[HALF:C, :], tilt_ref[0:HALF, :]], axis=0)
+    for half, block in enumerate((tilt_ref[...], turned)):
         block = jnp.concatenate([block, jnp.zeros((C, CP - C), F32)], axis=1)
-        high, low = split(block)
-        tilt_hi[half * CP : half * CP + C, :] = high
-        tilt_lo[half * CP : half * CP + C, :] = low
+        for which, value in enumerate(split(block)):
+            at = slice(which * CP, (which + 1) * CP)
+            tilt_in[half * CP : half * CP + C, at] = value
+            tilt_in[half * CP + C : (half + 1) * CP, at] = zeros_pad
+
+    def halves_sum(r, width):
+        return r[0:SD, 0:width] + r[SD : 2 * SD, 0:width] + r[0:SD, width : 2 * width]
 
     def to_frame(x):
-        high, low = split(jnp.concatenate([x * cos_az, x * sin_az], axis=1))
-        both = dot(jnp.concatenate([high, low], axis=0), tilt_hi[...])
-        return both[0:SD] + both[SD : 2 * SD] + dot(high, tilt_lo[...])
+        parts = split(jnp.concatenate([x * cos_az, x * sin_az], axis=1))
+        return halves_sum(dot(jnp.concatenate(parts, axis=0), tilt_in[...]), CP)
 
     def from_frame(x):
-        high, low = split(x)
-        both = dot_nt(jnp.concatenate([high, low], axis=0), tilt_hi[...])
-        u = both[0:SD] + both[SD : 2 * SD] + dot_nt(high, tilt_lo[...])
+        u = halves_sum(dot(jnp.concatenate(split(x), axis=0), tilt_out[...]), 2 * CP)
         return (u[:, 0:CP] * cos_az + u[:, CP : 2 * CP] * sin_az) * root
 
-    my_rows = pl.ds(pl.multiple_of(slot * SD, SD), SD)
+    def keep(a, h, framed):
+        def put(row, value):
+            field[a, h, plane, row : row + value.shape[0], :] = value
+
+        pack(put, framed)
+
     with jax.named_scope("frame0"):
         for h in range(2):
             v = jnp.concatenate([vec_ref[:, h, :], jnp.zeros((SD, CP - C), F32)], axis=1)
             vec[h] = v
-            field[0, h, my_rows, :] = to_frame(v)
+            keep(0, h, to_frame(v))
 
     with jax.named_scope("barrier_wait"):
         pl.semaphore_wait(barrier, 2 * (LINE - 1) + NZ * NC - 1)
 
-    def src_copy(peer):
-        return remote(geo_src_out, geo_src.at[slot], geo_src_send, geo_src_recv, peer)
+    def src_copy(peer, other):
+        to = geo_src.at[LINE * other + plane]
+        return remote(geo_src_out, to, geo_src_send, geo_src_recv, peer)
 
     src_all_copies = remote(
         geo_src.at[pl.ds(0, LINE * NC - 1)], geo_src.at[pl.ds(0, LINE * NC - 1)],
@@ -234,32 +275,39 @@
         return remote(flag_out.at[to], flag_in.at[j], flag_send, flag_recv.at[j], line_peer(j))
 
     def blocks(a, h, count, send, recv):
-        at = field.at[a, h, pl.ds(0, count * SD), :]
+        at = field.at[a, h, pl.ds(0, count), pl.ds(0, PACKED), :]
         return remote(at, at, send, recv, partner)
 
+    def packed_block(a, h, k):
+        return field.at[a, h, k, pl.ds(0, PACKED), :]
+
     def field_copy(a, h, ring, offset):
-        at = field.at[a, h, my_rows, :]
-        return remote(
-            at, at, field_send.at[a, h], field_recv.at[a, h, ring], plane_peer(offset, 1 - mc)
-        )
+        at = packed_block(a, h, plane)
+        return remote(at, at, field_send.at[a, h], field_recv.at[a, h, ring], plane_peer(offset, mc))
 
     def pair_copy(a, h, offset):
         source = lax.rem(mx + NX - offset[0], NX) * NY + lax.rem(my + NY - offset[1], NY)
-        core = mc if offset == (0, 0) else 1 - mc
-        rows = pl.ds(pl.multiple_of((source * NC + core) * SD, SD), SD)
-        at = field.at[a, h, rows, :]
-        return remote(at, at, pair_send.at[a, h], pair_recv.at[a, h], partner)
+        return remote(
+            packed_block(a, h, source), packed_block(a, h, LINE + source), pair_send.at[a, h], pair_recv.at[a, h],
+            partner,
+        )
 
     def send_part(a, h):
+        for z in range(NZ):
+
+            def put(row, value):
+                part_out[a, h, z, row : row + value.shape[0], :] = value
+
+            pack(put, part[z * SD : (z + 1) * SD, :])
         for k, j in enumerate(LINE_ORDER):
-            to = pl.ds(pl.multiple_of(lax.rem(mz + j, NZ) * SD, SD), SD)
             remote(
-                part.at[a, h, to, :], got.at[a, h, k], part_send.at[a, h], part_recv.at[a, h],
-                line_peer(j),
+                part_out.at[a, h, lax.rem(mz + j, NZ), pl.ds(0, PACKED), :],
+                got.at[a, h, k, pl.ds(0, PACKED), :],
+                part_send.at[a, h], part_recv.at[a, h], line_peer(j),
             ).start()
 
     def part_all(a, h):
-        at = got.at[a, h, pl.ds(0, NZ - 1)]
+        at = got.at[a, h, pl.ds(0, NZ - 1), pl.ds(0, PACKED), :]
         return remote(at, at, part_send.at[a, h], part_recv.at[a, h], partner)
 
     def send_pillar(r):
@@ -297,9 +345,9 @@
 
     with jax.named_scope("sends"):
         for offset in PLANE_ORDER:
-            for core in range(NC):
-                src_copy(plane_peer(offset, core)).start()
-        src_copy(partner).start()
+            for other in range(NC):
+                src_copy(plane_peer(offset, 1 - mc if other else mc), other).start()
+        src_copy(partner, 1).start()
         for j in LINE_ORDER:
             tgt_copy(j).start()
         for j in LINE_ORDER:
@@ -311,10 +359,16 @@
         loads[8].wait()
         for m in range(TERMS):
             block = jnp.concatenate([axial[m], jnp.zeros((C, CP - C), F32)], axis=1)
-            high, low = split(block)
-            for ref, value in ((ax_hi, high), (ax_lo, low)):
-                ref[m * CP : m * CP + C, :] = value
-                ref[m * CP + C : (m + 1) * CP, :] = zeros_pad
+            for which, value in enumerate(split(block)):
+                at = slice(which * CP, (which + 1) * CP)
+                ax_cat[m * CP : m * CP + C, at] = value
+                ax_cat[m * CP + C : (m + 1) * CP, at] = zeros_pad
+        for which in range(2):
+            for half in range(2):
+                at = (which * 2 + half) * CP
+                tilt_out[:, at : at + CP] = jnp.transpose(
+                    tilt_in[half * CP : (half + 1) * CP, which * CP : (which + 1) * CP].astype(F32)
+                ).astype(BF)
 
     with jax.named_scope("geo_wait"):
         src_all_copies.wait_recv()
@@ -329,11 +383,11 @@
     tgt_all = geo_tgt[0]
     for j in range(1, NZ):
         tgt_all = tgt_all + geo_tgt[j]
-    part[0, 0, :, 0:128] = jnp.transpose(jnp.concatenate([tgt_all] * 16, axis=0))
+    part[:, 0:128] = jnp.transpose(jnp.concatenate([tgt_all] * 16, axis=0))
 
     def weigh(flags, z):
         rows = pl.ds(pl.multiple_of(z * SD, SD), SD)
-        tgt = part[0, 0, rows, 0:128]
+        tgt = part[rows, 0:128]
         dx = tgt[:, 0:1] - src_all[0:1, :]
         dy = tgt[:, 1:2] - src_all[1:2, :]
         dz = tgt[:, 2:3] - src_all[2:3, :]
@@ -349,8 +403,10 @@
             wave = cos_d * float(np.cos(phase_step * m)) - sin_d * float(np.sin(phase_step * m))
             high, low = split(wave * scale)
             at = pl.ds(pl.multiple_of(m * TGT + z * SD, SD), SD)
-            w_hi[at, :] = high
-            w_lo[at, :] = low
+            for side in range(2):
+                for k, value in enumerate((high, high, low)):
+                    to = (3 * side + k) * 256
+                    w_cat[at, to : to + 256] = value[:, side * 256 : (side + 1) * 256]
 
     with jax.named_scope("weigh"):
         weigh(flag_out[mz], mz)
@@ -360,40 +416,9 @@
             weigh(flag_in[j], lax.rem(mz + NZ - j, NZ))
             return carry
 
-        for ring, (lo, hi) in enumerate(((1, 5), (5, 7), (7, 8))):
+        for ring, (lo, hi) in enumerate(((1, 3), (3, 6), (6, 8))):
+            relay(0, 0, ring)
             lax.fori_loop(lo, hi, weigh_from, 0)
-            relay(0, 0, ring)
-
-    def couple(a, h):
-        with jax.named_scope(f"gather_wait{a}{h}"):
-            blocks(a, h, LINE, pair_send.at[a, h], pair_recv.at[a, h]).wait_recv()
-        with jax.named_scope(f"first{a}{h}"):
-            high, low = split(field[a, h])
-            f_hi[...] = high
-            f_lo[...] = low
-            for block in range(2):
-                at = slice(block * 512, (block + 1) * 512)
-                g = dot(w_hi[at, :], f_hi[...]) + dot(w_hi[at, :], f_lo[...]) + dot(w_lo[at, :], f_hi[...])
-                g_high, g_low = split(g)
-                for k in range(4):
-                    m = block * 4 + k
-                    g_lhs[0:TGT, m * CP : (m + 1) * CP] = g_high[k * TGT : (k + 1) * TGT]
-                    g_lhs[TGT : 2 * TGT, m * CP : (m + 1) * CP] = g_low[k * TGT : (k + 1) * TGT]
-        if h == 0:
-            for ring in range(len(RINGS)):
-                relay(a, 1, ring)
-        with jax.named_scope(f"second{a}{h}"):
-            both = dot(g_lhs[...], ax_hi[...])
-            part[a, h] = both[0:TGT] + both[TGT : 2 * TGT] + dot(g_lhs[0:TGT, :], ax_lo[...])
-            send_part(a, h)
-
-    def collect(a, h):
-        total = part[a, h, pl.ds(pl.multiple_of(mz * SD, SD), SD), :]
-        with jax.named_scope(f"part_wait{a}{h}"):
-            part_all(a, h).wait_recv()
-        for k in range(NZ - 1):
-            total = total + got[a, h, k]
-        return from_frame(total)
 
     def reduce_pillar(r):
         with jax.named_scope(f"pillar_wait{r}"):
@@ -412,12 +437,72 @@
             total = total + scal_b[r, k]
         return jnp.sum(total, axis=1, keepdims=True)
 
+    def couple(a, h):
+        def unfold(side):
+            for k in range(LINE):
+                tiles = [field[a, h, LINE * side + k, 8 * t : 8 * t + 8, :] for t in range(5)]
+                tail = field[a, h, LINE * side + k, 40:42, :]
+                high, low = split(unpack(tiles, tail))
+                for t, value in enumerate((high, low, high)):
+                    row = (3 * side + t) * 256 + k * SD
+                    f_cat[row : row + SD, :] = value
+
+        def arrive():
+            with jax.named_scope(f"gather_wait{a}{h}"):
+                blocks(a, h, LINE, pair_send.at[a, h], pair_recv.at[a, h]).wait_recv()
+
+        if h == 1:
+            arrive()
+        with jax.named_scope(f"early{a}{h}"):
+            unfold(0)
+            if h == 0:
+                for piece in range(2):
+                    at = slice(piece * 512, (piece + 1) * 512)
+                    g_acc[at, :] = dot(w_cat[at, 0:768], f_cat[0:768, :])
+        if h == 0:
+            arrive()
+        with jax.named_scope(f"first{a}{h}"):
+            unfold(1)
+            for piece in range(2):
+                at = slice(piece * 512, (piece + 1) * 512)
+                if h == 0:
+                    g = g_acc[at, :] + dot(w_cat[at, 768:1536], f_cat[768:1536, :])
+                else:
+                    g = dot(w_cat[at, :], f_cat[...])
+                g_high, g_low = split(g)
+                for k in range(4):
+                    m = piece * 4 + k
+                    g_lhs[0:TGT, m * CP : (m + 1) * CP] = g_high[k * TGT : (k + 1) * TGT]
+                    g_lhs[TGT : 2 * TGT, m * CP : (m + 1) * CP] = g_low[k * TGT : (k + 1) * TGT]
+        if h == 0:
+            for ring in range(len(RINGS)):
+                relay(a, 1, ring)
+            if a == 1:
+                reduce_pillar(0)
+        with jax.named_scope(f"second{a}{h}"):
+            both = dot(g_lhs[...], ax_cat[:, 0:CP])
+            part[...] = both[0:TGT] + both[TGT : 2 * TGT] + dot(g_lhs[0:TGT, :], ax_cat[:, CP : 2 * CP])
+            send_part(a, h)
+
+    def collect(a, h):
+        with jax.named_scope(f"part_wait{a}{h}"):
+            part_all(a, h).wait_recv()
+
+        def summed(lo, hi):
+            total = part_out[a, h, mz, lo:hi, :]
+            for k in range(NZ - 1):
+                total = total + got[a, h, k, lo:hi, :]
+            return total
+
+        total = unpack([summed(8 * t, 8 * t + 8) for t in range(5)], summed(40, 42))
+        return from_frame(total)
+
     couple(0, 0)
     couple(0, 1)
     for h in range(2):
         image = vec[h] - collect(0, h)
         img[h] = image
-        field[1, h, my_rows, :] = to_frame(image)
+        keep(1, h, to_frame(image))
         send_field(1, h)
 
     scal_out[...] = jnp.zeros((2, 8, 128), F32)
@@ -427,8 +512,8 @@
     for ring in range(len(RINGS)):
         relay(1, 0, ring)
     couple(1, 0)
-    reduce_pillar(0)
     couple(1, 1)
+    seconds = [img[h] - collect(1, h) for h in range(2)]
     sums = reduce_plane(0)
     rho_start = sums[0:1, :]
     alpha = rho_start / sums[1:2, :]
@@ -440,9 +525,8 @@
     half_image = []
     for h in range(2):
         image = img[h]
-        second = image - collect(1, h)
         half_step.append(vec[h] - alpha * image)
-        half_image.append(image - alpha * second)
+        half_image.append(image - alpha * seconds[h])
     right = [vec[0], vec[1]]
     scal_out[1, 0:1, :] = inner(half_image, half_step)
     scal_out[1, 1:2, :] = inner(half_image, half_image)
@@ -475,8 +559,12 @@
 
 
 def put_out(*refs):
-    for k in range(3):
-        refs[3 + k][...] = refs[k][...]
+    ins, outs, sems = refs[:3], refs[3:6], refs[6]
+    copies = [pltpu.make_async_copy(a, b, sems.at[k]) for k, (a, b) in enumerate(zip(ins, outs))]
+    for copy in copies:
+        copy.start()
+    for copy in copies:
+        copy.wait()
 
 
 def on_device(
@@ -504,10 +592,9 @@
                 V((C, C), F32),
                 V((TERMS, C, C), F32),
                 V((8, CP), F32),
-                V((TERMS * CP, CP), BF),
-                V((TERMS * CP, CP), BF),
-                V((2 * CP, CP), BF),
-                V((2 * CP, CP), BF),
+                V((TERMS * CP, 2 * CP), BF),
+                V((2 * CP, 2 * CP), BF),
+                V((CP, 4 * CP), BF),
                 V((NZ, SD, SRC), jnp.int32),
                 V((NZ, SD, SRC), jnp.int32),
                 V((8, 128), F32),
@@ -515,14 +602,14 @@
                 V((8, 128), F32),
                 V((LINE * NC, 8, 128), F32),
                 V((NZ, 8, 128), F32),
-                V((TERMS * TGT, SRC), BF),
-                V((TERMS * TGT, SRC), BF),
-                V((2, 2, SRC, CP), F32),
-                V((SRC, CP), BF),
-                V((SRC, CP), BF),
+                V((TERMS * TGT, 3 * SRC), BF),
+                V((2, 2, LINE * NC, 48, 128), F32),
+                V((3 * SRC, CP), BF),
                 V((2 * TGT, TERMS * CP), BF),
-                V((2, 2, TGT, CP), F32),
-                V((2, 2, NZ, SD, CP), F32),
+                V((TERMS * TGT, CP), F32),
+                V((TGT, CP), F32),
+                V((2, 2, NZ, 48, 128), F32),
+                V((2, 2, NZ, 48, 128), F32),
                 V((2, SD, CP), F32),
                 V((2, SD, CP), F32),
                 V((2, SD, CP), F32),
@@ -549,18 +636,23 @@
                 dma((2,)),
             ],
             compiler_params=pltpu.CompilerParams(
-                collective_id=0, has_side_effects=True
+                collective_id=0, has_side_effects=True, vmem_limit_bytes=48 * 1024 * 1024
             ),
         )(
-            right_side,
-            positions,
-            sphere_radii.reshape(1, SD),
-            azimuths.reshape(1, SD),
-            pair_flags,
-            pair_counts.reshape(1, SD),
-            tilt_matrix,
-            axial_terms,
-            jnp.asarray(orders_rows()),
+            *(
+                pltpu.with_memory_space_constraint(x, pltpu.HBM)
+                for x in (
+                    right_side,
+                    positions,
+                    sphere_radii.reshape(1, SD),
+                    azimuths.reshape(1, SD),
+                    pair_flags,
+                    pair_counts.reshape(1, SD),
+                    tilt_matrix,
+                    axial_terms,
+                    jnp.asarray(orders_rows()),
+                )
+            )
         )
     )
     return tuple(
@@ -569,7 +661,9 @@
             name="put_out",
             out_shape=(out, out, out),
             in_specs=[vmem] * 3,
-            out_specs=(vmem,) * 3,
+            out_specs=(hbm,) * 3,
+            scratch_shapes=[dma((3,))],
+            compiler_params=pltpu.CompilerParams(vmem_limit_bytes=2 * 1024 * 1024),
         )(*results)
     )
 

time: 69.9 us -> 64.2 us (0.918)
  Pallas kernels: 69.1 us -> 63.3 us
    pallas_call x1, Pallas kernels: 67.6 us -> 62.6 us  [on_device(): pl.pallas_call(kernel, name='bicgstab', out_shape=(out, out, out), in_spe...]
    pallas_call x1, Pallas kernels: 1.52 us -> 0.68 us  [on_device(): pl.pallas_call(put_out, name='put_out', out_shape=(out, out, out), in_spe...]
where the time goes in v3:
time: 64.2 us; the launch traced here: 64.1 us
  Pallas kernels  63.3 us (99%)
  between operations  0.8 us (1%)
    pallas_call x1, Pallas kernels, on_device(): pl.pallas_call(kernel, name='bicgstab', out_shape=(out, out, out), in_spe...  62.6 us

profile of v3, /device:TPU:1, one launch (start us, length us, event | category | flops | bytes accessed | tf_op | source)
XLA Modules:
  0.0 64.1 jit_solution(7776362933418196641)
XLA Ops:
  0.6 62.6 %bicgstab.1 = (f32[16,2,336]{2,1,0:T(2,128)S(1)}, f32[16,2,336]{2,1,0:T(2,128)S(1)}, f32[16,2,336]{2,1,0:T(2,128)S(1)}) custom-call(f32[16,2,336]{2,1,0:T(2,128)} %vec_hbm.1, f32[3,16]{1,0:T(4,128)} %pos_hbm.1, f32[1,16]{1,0:T(1,128)} %bitcast.3, f32[1,16]{1,0:T(1,128)} %bitcast.4, s32[16,4096]{1,0:T(8,128)} %flags_hbm.1, s32[1,16]{1,0:T(1,128)} %bitcast.5, ...), custom_call_target="tpu_custom_call" | custom-call | tf_op jit(solution)/shard_map/bicgstab/pallas_call | solution.py:579
  63.2 0.7 %put_out.1 = (f32[16,2,336]{2,1,0:T(2,128)}, f32[16,2,336]{2,1,0:T(2,128)}, f32[16,2,336]{2,1,0:T(2,128)}) custom-call(f32[16,2,336]{2,1,0:T(2,128)S(1)} %get-tuple-element.6.refs_0_, f32[16,2,336]{2,1,0:T(2,128)S(1)} %get-tuple-element.7.refs_1_, f32[16,2,336]{2,1,0:T(2,128)S(1)} %get-tuple-element.8.refs_2_), custom_call_target="tpu_custom_call" | custom-call | tf_op jit(solution)/shard_map/put_out/pallas_call | solution.py:659

commit v4 on v3

--- a/solution.py
+++ b/solution.py
@@ -211,6 +211,109 @@
                         at = 128 * (2 * side + eight)
                         flag_out[4 * upper + r, :, at : at + 128] = tile
 
+    with jax.named_scope("barrier_wait"):
+        pl.semaphore_wait(barrier, 2 * (LINE - 1) + NZ * NC - 1)
+
+    def src_copy(peer, other):
+        to = geo_src.at[LINE * other + plane]
+        return remote(geo_src_out, to, geo_src_send, geo_src_recv, peer)
+
+    src_all_copies = remote(
+        geo_src.at[pl.ds(0, LINE * NC - 1)], geo_src.at[pl.ds(0, LINE * NC - 1)],
+        geo_src_send, geo_src_recv, partner,
+    )
+
+    def tgt_copy(j):
+        return remote(geo_tgt_out, geo_tgt.at[j], geo_tgt_send, geo_tgt_recv, line_peer(j))
+
+    tgt_all_copies = remote(
+        geo_tgt.at[pl.ds(0, NZ - 1)], geo_tgt.at[pl.ds(0, NZ - 1)],
+        geo_tgt_send, geo_tgt_recv, partner,
+    )
+
+    def flag_copy(j):
+        to = lax.rem(mz + j, NZ)
+        return remote(flag_out.at[to], flag_in.at[j], flag_send, flag_recv.at[j], line_peer(j))
+
+    def blocks(a, h, count, send, recv):
+        at = field.at[a, h, pl.ds(0, count), pl.ds(0, PACKED), :]
+        return remote(at, at, send, recv, partner)
+
+    def packed_block(a, h, k):
+        return field.at[a, h, k, pl.ds(0, PACKED), :]
+
+    def field_copy(a, h, ring, offset):
+        at = packed_block(a, h, plane)
+        return remote(at, at, field_send.at[a, h], field_recv.at[a, h, ring], plane_peer(offset, mc))
+
+    def pair_copy(a, h, offset):
+        source = lax.rem(mx + NX - offset[0], NX) * NY + lax.rem(my + NY - offset[1], NY)
+        return remote(
+            packed_block(a, h, source), packed_block(a, h, LINE + source), pair_send.at[a, h], pair_recv.at[a, h],
+            partner,
+        )
+
+    def send_part(a, h):
+        for z in range(NZ):
+
+            def put(row, value):
+                part_out[a, h, z, row : row + value.shape[0], :] = value
+
+            pack(put, part[z * SD : (z + 1) * SD, :])
+        for k, j in enumerate(LINE_ORDER):
+            remote(
+                part_out.at[a, h, lax.rem(mz + j, NZ), pl.ds(0, PACKED), :],
+                got.at[a, h, k, pl.ds(0, PACKED), :],
+                part_send.at[a, h], part_recv.at[a, h], line_peer(j),
+            ).start()
+
+    def part_all(a, h):
+        at = got.at[a, h, pl.ds(0, NZ - 1), pl.ds(0, PACKED), :]
+        return remote(at, at, part_send.at[a, h], part_recv.at[a, h], partner)
+
+    def send_pillar(r):
+        for k, (j, core) in enumerate(PILLAR_ORDER):
+            remote(
+                scal_out.at[r], scal_a.at[r, k], sa_send.at[r], sa_recv.at[r], pillar_peer(j, core)
+            ).start()
+
+    def sa_all(r):
+        at = scal_a.at[r, pl.ds(0, NZ * NC - 1)]
+        return remote(at, at, sa_send.at[r], sa_recv.at[r], partner)
+
+    def send_plane(r):
+        for k, offset in enumerate(PLANE_ORDER):
+            remote(
+                scal_mid.at[r], scal_b.at[r, k], sb_send.at[r], sb_recv.at[r],
+                plane_peer(offset, mc),
+            ).start()
+
+    def sb_all(r):
+        at = scal_b.at[r, pl.ds(0, LINE - 1)]
+        return remote(at, at, sb_send.at[r], sb_recv.at[r], partner)
+
+    def send_field(a, h):
+        for ring, offsets in enumerate(RINGS):
+            for offset in offsets:
+                field_copy(a, h, ring, offset).start()
+        pair_copy(a, h, (0, 0)).start()
+
+    def relay(a, h, ring):
+        with jax.named_scope(f"relay{a}{h}{ring}"):
+            blocks(a, h, len(RINGS[ring]), field_send.at[a, h], field_recv.at[a, h, ring]).wait_recv()
+            for offset in RINGS[ring]:
+                pair_copy(a, h, offset).start()
+
+    with jax.named_scope("sends"):
+        for j in LINE_ORDER:
+            tgt_copy(j).start()
+        for offset in PLANE_ORDER:
+            for other in range(NC):
+                src_copy(plane_peer(offset, 1 - mc if other else mc), other).start()
+        src_copy(partner, 1).start()
+        for j in LINE_ORDER:
+            flag_copy(j).start()
+
     loads[6].wait()
     loads[7].wait()
     cols = jnp.transpose(jnp.concatenate([own] * 16, axis=0))
@@ -250,108 +353,7 @@
             vec[h] = v
             keep(0, h, to_frame(v))
 
-    with jax.named_scope("barrier_wait"):
-        pl.semaphore_wait(barrier, 2 * (LINE - 1) + NZ * NC - 1)
-
-    def src_copy(peer, other):
-        to = geo_src.at[LINE * other + plane]
-        return remote(geo_src_out, to, geo_src_send, geo_src_recv, peer)
-
-    src_all_copies = remote(
-        geo_src.at[pl.ds(0, LINE * NC - 1)], geo_src.at[pl.ds(0, LINE * NC - 1)],
-        geo_src_send, geo_src_recv, partner,
-    )
-
-    def tgt_copy(j):
-        return remote(geo_tgt_out, geo_tgt.at[j], geo_tgt_send, geo_tgt_recv, line_peer(j))
-
-    tgt_all_copies = remote(
-        geo_tgt.at[pl.ds(0, NZ - 1)], geo_tgt.at[pl.ds(0, NZ - 1)],
-        geo_tgt_send, geo_tgt_recv, partner,
-    )
-
-    def flag_copy(j):
-        to = lax.rem(mz + j, NZ)
-        return remote(flag_out.at[to], flag_in.at[j], flag_send, flag_recv.at[j], line_peer(j))
-
-    def blocks(a, h, count, send, recv):
-        at = field.at[a, h, pl.ds(0, count), pl.ds(0, PACKED), :]
-        return remote(at, at, send, recv, partner)
-
-    def packed_block(a, h, k):
-        return field.at[a, h, k, pl.ds(0, PACKED), :]
-
-    def field_copy(a, h, ring, offset):
-        at = packed_block(a, h, plane)
-        return remote(at, at, field_send.at[a, h], field_recv.at[a, h, ring], plane_peer(offset, mc))
-
-    def pair_copy(a, h, offset):
-        source = lax.rem(mx + NX - offset[0], NX) * NY + lax.rem(my + NY - offset[1], NY)
-        return remote(
-            packed_block(a, h, source), packed_block(a, h, LINE + source), pair_send.at[a, h], pair_recv.at[a, h],
-            partner,
-        )
-
-    def send_part(a, h):
-        for z in range(NZ):
-
-            def put(row, value):
-                part_out[a, h, z, row : row + value.shape[0], :] = value
-
-            pack(put, part[z * SD : (z + 1) * SD, :])
-        for k, j in enumerate(LINE_ORDER):
-            remote(
-                part_out.at[a, h, lax.rem(mz + j, NZ), pl.ds(0, PACKED), :],
-                got.at[a, h, k, pl.ds(0, PACKED), :],
-                part_send.at[a, h], part_recv.at[a, h], line_peer(j),
-            ).start()
-
-    def part_all(a, h):
-        at = got.at[a, h, pl.ds(0, NZ - 1), pl.ds(0, PACKED), :]
-        return remote(at, at, part_send.at[a, h], part_recv.at[a, h], partner)
-
-    def send_pillar(r):
-        for k, (j, core) in enumerate(PILLAR_ORDER):
-            remote(
-                scal_out.at[r], scal_a.at[r, k], sa_send.at[r], sa_recv.at[r], pillar_peer(j, core)
-            ).start()
-
-    def sa_all(r):
-        at = scal_a.at[r, pl.ds(0, NZ * NC - 1)]
-        return remote(at, at, sa_send.at[r], sa_recv.at[r], partner)
-
-    def send_plane(r):
-        for k, offset in enumerate(PLANE_ORDER):
-            remote(
-                scal_mid.at[r], scal_b.at[r, k], sb_send.at[r], sb_recv.at[r],
-                plane_peer(offset, mc),
-            ).start()
-
-    def sb_all(r):
-        at = scal_b.at[r, pl.ds(0, LINE - 1)]
-        return remote(at, at, sb_send.at[r], sb_recv.at[r], partner)
-
-    def send_field(a, h):
-        for ring, offsets in enumerate(RINGS):
-            for offset in offsets:
-                field_copy(a, h, ring, offset).start()
-        pair_copy(a, h, (0, 0)).start()
-
-    def relay(a, h, ring):
-        with jax.named_scope(f"relay{a}{h}{ring}"):
-            blocks(a, h, len(RINGS[ring]), field_send.at[a, h], field_recv.at[a, h, ring]).wait_recv()
-            for offset in RINGS[ring]:
-                pair_copy(a, h, offset).start()
-
-    with jax.named_scope("sends"):
-        for offset in PLANE_ORDER:
-            for other in range(NC):
-                src_copy(plane_peer(offset, 1 - mc if other else mc), other).start()
-        src_copy(partner, 1).start()
-        for j in LINE_ORDER:
-            tgt_copy(j).start()
-        for j in LINE_ORDER:
-            flag_copy(j).start()
+    with jax.named_scope("send_fields"):
         send_field(0, 0)
         send_field(0, 1)
 
@@ -411,7 +413,8 @@
     with jax.named_scope("weigh"):
         weigh(flag_out[mz], mz)
 
-        def weigh_from(j, carry):
+        def weigh_from(k, carry):
+            j = 4 + (k // 2) * (2 * lax.rem(k, 2) - 1)
             flag_copy(j).wait_recv()
             weigh(flag_in[j], lax.rem(mz + NZ - j, NZ))
             return carry
@@ -451,21 +454,22 @@
             with jax.named_scope(f"gather_wait{a}{h}"):
                 blocks(a, h, LINE, pair_send.at[a, h], pair_recv.at[a, h]).wait_recv()
 
-        if h == 1:
+        split_phases = h == 0 or a == 1
+        if not split_phases:
             arrive()
         with jax.named_scope(f"early{a}{h}"):
             unfold(0)
-            if h == 0:
+            if split_phases:
                 for piece in range(2):
                     at = slice(piece * 512, (piece + 1) * 512)
                     g_acc[at, :] = dot(w_cat[at, 0:768], f_cat[0:768, :])
-        if h == 0:
+        if split_phases:
             arrive()
         with jax.named_scope(f"first{a}{h}"):
             unfold(1)
             for piece in range(2):
                 at = slice(piece * 512, (piece + 1) * 512)
-                if h == 0:
+                if split_phases:
                     g = g_acc[at, :] + dot(w_cat[at, 768:1536], f_cat[768:1536, :])
                 else:
                     g = dot(w_cat[at, :], f_cat[...])
@@ -474,15 +478,17 @@
                     m = piece * 4 + k
                     g_lhs[0:TGT, m * CP : (m + 1) * CP] = g_high[k * TGT : (k + 1) * TGT]
                     g_lhs[TGT : 2 * TGT, m * CP : (m + 1) * CP] = g_low[k * TGT : (k + 1) * TGT]
-        if h == 0:
+        if h == 0 and a == 0:
             for ring in range(len(RINGS)):
-                relay(a, 1, ring)
-            if a == 1:
-                reduce_pillar(0)
+                relay(0, 1, ring)
         with jax.named_scope(f"second{a}{h}"):
             both = dot(g_lhs[...], ax_cat[:, 0:CP])
             part[...] = both[0:TGT] + both[TGT : 2 * TGT] + dot(g_lhs[0:TGT, :], ax_cat[:, CP : 2 * CP])
             send_part(a, h)
+        if h == 0 and a == 1:
+            for ring in range(len(RINGS)):
+                relay(1, 1, ring)
+            reduce_pillar(0)
 
     def collect(a, h):
         with jax.named_scope(f"part_wait{a}{h}"):

time: 64.2 us -> 63.2 us (0.984)
  Pallas kernels: 63.3 us -> 62.3 us
    pallas_call x1, Pallas kernels: 62.6 us -> 61.6 us  [on_device(): pl.pallas_call(kernel, name='bicgstab', out_shape=(out, out, out), in_spe...]
where the time goes in v4:
time: 63.2 us; the launch traced here: 63.1 us
  Pallas kernels  62.3 us (99%)
  between operations  0.8 us (1%)
    pallas_call x1, Pallas kernels, on_device(): pl.pallas_call(kernel, name='bicgstab', out_shape=(out, out, out), in_spe...  61.6 us

profile of v4, /device:TPU:1, one launch (start us, length us, event | category | flops | bytes accessed | tf_op | source)
XLA Modules:
  0.0 63.1 jit_solution(3092315311880121282)
XLA Ops:
  0.6 61.6 %bicgstab.1 = (f32[16,2,336]{2,1,0:T(2,128)S(1)}, f32[16,2,336]{2,1,0:T(2,128)S(1)}, f32[16,2,336]{2,1,0:T(2,128)S(1)}) custom-call(f32[16,2,336]{2,1,0:T(2,128)} %vec_hbm.1, f32[3,16]{1,0:T(4,128)} %pos_hbm.1, f32[1,16]{1,0:T(1,128)} %bitcast.3, f32[1,16]{1,0:T(1,128)} %bitcast.4, s32[16,4096]{1,0:T(8,128)} %flags_hbm.1, s32[1,16]{1,0:T(1,128)} %bitcast.5, ...), custom_call_target="tpu_custom_call" | custom-call | tf_op jit(solution)/shard_map/bicgstab/pallas_call | solution.py:585
  62.3 0.7 %put_out.1 = (f32[16,2,336]{2,1,0:T(2,128)}, f32[16,2,336]{2,1,0:T(2,128)}, f32[16,2,336]{2,1,0:T(2,128)}) custom-call(f32[16,2,336]{2,1,0:T(2,128)S(1)} %get-tuple-element.6.refs_0_, f32[16,2,336]{2,1,0:T(2,128)S(1)} %get-tuple-element.7.refs_1_, f32[16,2,336]{2,1,0:T(2,128)S(1)} %get-tuple-element.8.refs_2_), custom_call_target="tpu_custom_call" | custom-call | tf_op jit(solution)/shard_map/put_out/pallas_call | solution.py:665

commit v5 on v4

--- a/solution.py
+++ b/solution.py
@@ -519,25 +519,24 @@
         relay(1, 0, ring)
     couple(1, 0)
     couple(1, 1)
-    seconds = [img[h] - collect(1, h) for h in range(2)]
+    first_second = img[0] - collect(1, 0)
     sums = reduce_plane(0)
     rho_start = sums[0:1, :]
     alpha = rho_start / sums[1:2, :]
-
-    def inner(left, right):
-        return lanes_of(left[0] * right[0] + left[1] * right[1])
-
-    half_step = []
-    half_image = []
-    for h in range(2):
-        image = img[h]
-        half_step.append(vec[h] - alpha * image)
-        half_image.append(image - alpha * seconds[h])
     right = [vec[0], vec[1]]
-    scal_out[1, 0:1, :] = inner(half_image, half_step)
-    scal_out[1, 1:2, :] = inner(half_image, half_image)
-    scal_out[1, 2:3, :] = inner(right, half_step)
-    scal_out[1, 3:4, :] = inner(right, half_image)
+    half_step = [right[h] - alpha * img[h] for h in range(2)]
+    half_image = [img[0] - alpha * first_second]
+
+    def products(h):
+        return (
+            half_image[h] * half_step[h], half_image[h] * half_image[h],
+            right[h] * half_step[h], right[h] * half_image[h],
+        )
+
+    early = [lanes_of(value) for value in products(0)]
+    half_image.append(img[1] - alpha * (img[1] - collect(1, 1)))
+    for row, value in enumerate(products(1)):
+        scal_out[1, row : row + 1, :] = early[row] + lanes_of(value)
     send_pillar(1)
     reduce_pillar(1)
     sums = reduce_plane(1)

time: 63.2 us -> 63.1 us (level)
  no operation moved by 1% of the time
where the time goes in v5:
time: 63.1 us; the launch traced here: 63 us
  Pallas kernels  62.2 us (99%)
  between operations  0.8 us (1%)
    pallas_call x1, Pallas kernels, on_device(): pl.pallas_call(kernel, name='bicgstab', out_shape=(out, out, out), in_spe...  61.5 us

profile of v5, /device:TPU:1, one launch (start us, length us, event | category | flops | bytes accessed | tf_op | source)
XLA Modules:
  0.0 63.0 jit_solution(7882452557529270812)
XLA Ops:
  0.6 61.5 %bicgstab.1 = (f32[16,2,336]{2,1,0:T(2,128)S(1)}, f32[16,2,336]{2,1,0:T(2,128)S(1)}, f32[16,2,336]{2,1,0:T(2,128)S(1)}) custom-call(f32[16,2,336]{2,1,0:T(2,128)} %vec_hbm.1, f32[3,16]{1,0:T(4,128)} %pos_hbm.1, f32[1,16]{1,0:T(1,128)} %bitcast.3, f32[1,16]{1,0:T(1,128)} %bitcast.4, s32[16,4096]{1,0:T(8,128)} %flags_hbm.1, s32[1,16]{1,0:T(1,128)} %bitcast.5, ...), custom_call_target="tpu_custom_call" | custom-call | tf_op jit(solution)/shard_map/bicgstab/pallas_call | solution.py:584
  62.1 0.7 %put_out.1 = (f32[16,2,336]{2,1,0:T(2,128)}, f32[16,2,336]{2,1,0:T(2,128)}, f32[16,2,336]{2,1,0:T(2,128)}) custom-call(f32[16,2,336]{2,1,0:T(2,128)S(1)} %get-tuple-element.6.refs_0_, f32[16,2,336]{2,1,0:T(2,128)S(1)} %get-tuple-element.7.refs_1_, f32[16,2,336]{2,1,0:T(2,128)S(1)} %get-tuple-element.8.refs_2_), custom_call_target="tpu_custom_call" | custom-call | tf_op jit(solution)/shard_map/put_out/pallas_call | solution.py:664
